TPU v7x, 8 devices: a whole 2x2x1 slice. The times are simulated.
8 devices in a mesh: dp: 2 (over z, y), tp: 4 (over x, core).
Axes of the slice: x: 2, y: 2, z: 1, core: 2. Of those that a mesh axis runs over, the one named last changes fastest.
Arguments:
- enc_out: bfloat16 [12, 2048, 2048], P('dp', 'tp'), parts along dimension 0
- norm_scale: bfloat16 [2048], replicated
- w_key: bfloat16 [6, 2048, 32, 64], P(None, None, 'tp')
- w_value: bfloat16 [6, 2048, 32, 64], P(None, None, 'tp')
Outputs:
- output 1: bfloat16 [6, 12, 2048, 32, 64], P(None, 'dp', None, 'tp'), parts along dimension 1
- output 2: bfloat16 [6, 12, 2048, 32, 64], P(None, 'dp', None, 'tp'), parts along dimension 1
There are 2 independent parts. A program takes and returns all parts, laid end to end along the dimension named above; an argument that names none is the same for every part.
All inputs are finite; a program needn't handle non-finite values.
Results may differ from a plain program's by a relative error of at most 0.001.
Values are sent between devices in bfloat16 or wider.
A program may use at most 1 GiB of HBM per device.

v0:
```python
import jax
import jax.numpy as jnp
from jax import lax
from jax.sharding import PartitionSpec as P

NORM_EPS = 1e-6


def rms_norm(enc_out, norm_scale):
    acts = enc_out.astype(jnp.float32)
    mean_sq = jnp.mean(acts * acts, axis=-1, keepdims=True)
    return (acts * lax.rsqrt(mean_sq + NORM_EPS) * norm_scale.astype(jnp.float32)).astype(jnp.bfloat16)


def solution(mesh):
    def per_device(enc_out, norm_scale, w_key, w_value):
        normed = rms_norm(enc_out, norm_scale)
        gathered = lax.all_gather(normed, "tp", axis=1, tiled=True)
        key_cache = jnp.einsum("bsd,ldhk->lbshk", gathered, w_key, preferred_element_type=jnp.float32).astype(jnp.bfloat16)
        value_cache = jnp.einsum("bsd,ldhk->lbshk", gathered, w_value, preferred_element_type=jnp.float32).astype(jnp.bfloat16)
        return key_cache, value_cache

    weight_spec = P(None, None, "tp", None)
    cache_spec = P(None, "dp", None, "tp", None)
    return jax.shard_map(per_device, mesh=mesh, in_specs=(P("dp", "tp", None), P(None), weight_spec, weight_spec), out_specs=(cache_spec, cache_spec), check_vma=False)
```

profile of v0, /device:TPU:0, one launch (start us, length us, event | category | flops | bytes accessed | tf_op | source)
XLA Modules:
  0.0 765.3 jit_solution(16323129184945918817)
XLA Ops:
  7.2 0.0 all-gather.2.cloned.1.call-start
  7.2 0.7 convert_element_type.22
  7.9 7.1 fusion.8
  15.0 11.7 %fusion.10 = bf16[6,512,2048]{2,1,0:T(8,128)(2,1)} fusion(bf16[6,512,2048]{2,1,0:T(8,128)(2,1)} %param.4, f32[2048]{0:T(1024)S(1)} %convert_element_type.22, f32[6,512]{1,0:T(8,128)S(1)} %add_rsqrt_fusion), kind=kLoop, calls=%fused_computation.10 | loop fusion | flops 25165824 | bytes 25186304 | tf_op jit(solution)/shard_map/convert_element_type | solution.py:12
  26.7 0.0 all-gather.2.cloned.1.call-update
  26.7 297.5 %all-gather.2.cloned.1.call-done = bf16[6,2048,2048]{2,1,0:T(8,128)(2,1)} async-done(((bf16[6,512,2048]{2,1,0:T(8,128)(2,1)}), bf16[6,2048,2048]{2,1,0:T(8,128)(2,1)}) %all-gather.2.cloned.1.call-update) | async-done | bytes 50331664 | tf_op jit(solution)/shard_map/all_gather | solution.py:18
  324.2 167.7 %convert_bitcast_fusion = bf16[6,6,2048,8,64]{2,4,3,0,1:T(8,128)(2,1)} fusion(bf16[6,2048,2048]{2,1,0:T(8,128)(2,1)} %all-gather.2.cloned.1.call-done, bf16[6,2048,8,64]{1,3,2,0:T(8,128)(2,1)} %param.7), kind=kOutput, calls=%fused_computation | convolution fusion | flops 154656571392 | bytes 138412032 | tf_op jit(solution)/shard_map/bsd,ldhk->lbshk/dot_general | solution.py:20
  491.9 49.4 %copy.7 = bf16[6,6,2048,8,64]{2,4,3,1,0:T(8,128)(2,1)} copy(bf16[6,6,2048,8,64]{2,4,3,0,1:T(8,128)(2,1)} %convert_bitcast_fusion) | data formatting | bytes 150994944
  541.2 167.9 %convert_bitcast_fusion.1 = bf16[6,6,2048,8,64]{2,4,3,0,1:T(8,128)(2,1)} fusion(bf16[6,2048,2048]{2,1,0:T(8,128)(2,1)} %all-gather.2.cloned.1.call-done, bf16[6,2048,8,64]{1,3,2,0:T(8,128)(2,1)} %param.6), kind=kOutput, calls=%fused_computation.1 | convolution fusion | flops 154656571392 | bytes 138412032 | tf_op jit(solution)/shard_map/bsd,ldhk->lbshk/dot_general | solution.py:19
  709.1 49.4 %copy.6 = bf16[6,6,2048,8,64]{2,4,3,1,0:T(8,128)(2,1)} copy(bf16[6,6,2048,8,64]{2,4,3,0,1:T(8,128)(2,1)} %convert_bitcast_fusion.1) | data formatting | bytes 150994944
  (1 shorter events, 0.0 us)
Async XLA Ops:
  7.2 317.1 %all-gather.2.cloned.1.call-start = ((), (), s32[]{:S(2)}) async-start(), calls=%async_computation | async-start | bytes 62914560 | tf_op jit(solution)/shard_map/all_gather | solution.py:18
Sparse Core Ops, SparseCore 0:
  26.8 297.3 all-gather.1
where the time goes:
time: 766 us; the launch traced here: 765 us
  matrix products  336 us (44%)
  waiting for transfers between devices  298 us (39%)
  local copies, waits for them, and re-layouts  98.8 us (13%)
  other arithmetic  19.5 us (3%)
  between operations  14 us (2%)
    all_gather x1, waiting for transfers between devices, per_device(): gathered = lax.all_gather(normed, 'tp', axis=1, tiled=True)  297 us
    dot_general x1, matrix products, per_device(): jnp.einsum('bsd,ldhk->lbshk', gathered, w_key, preferred_element_type=jnp...  168 us
    dot_general x1, matrix products, per_device(): jnp.einsum('bsd,ldhk->lbshk', gathered, w_value, preferred_element_type=j...  168 us
    unnamed x2, local copies, waits for them, and re-layouts  98.8 us
  transfers between devices with their start and end apart: 1, of which 1 were waited for; matrix products, arithmetic and copies ran while one was open for 0% of the time, Pallas kernels for 0%

commit v1 on v0

v1 whole, which is shorter than its diff:
```python
import functools
import jax, jax.numpy as jnp
from jax import lax
from jax.experimental import pallas as pl
from jax.experimental.pallas import tpu as pltpu

from jax.sharding import PartitionSpec as P

NORM_EPS = 1e-6
L, D, HK, TOK = 6, 2048, 512, 512
PIECES, ROWS = 4, 128
NT = D // 256

def proj_body(units, n_src, has_prev, *refs):
    n = len(units)
    srcs = refs[:n_src]
    wk, wv = refs[n_src:n_src + 2]
    ok, ov = refs[n_src + 2 + (2 if has_prev else 0):n_src + 4 + (2 if has_prev else 0)]
    ybuf, wbuf, obuf, y_sem, w_sem, o_sem = refs[-6:]
    me = lax.axis_index("tp")

    def out_copy(kv, t, slot):
        t = jnp.maximum(t, 0)
        layer, u = t // n, t % n
        seq, code = unit_scalars(u)
        other = jnp.bitwise_xor(me, code)
        dst = (ok, ov)[kv].at[layer, seq, :, pl.ds(pl.multiple_of(other * TOK, TOK), TOK)]
        return pltpu.make_async_copy(obuf.at[kv, slot], dst, o_sem.at[kv])

    def unit_scalars(u):
        seq, code = jnp.int32(units[0][2]), jnp.int32(units[0][3])
        for i in range(1, n):
            seq = jnp.where(u == i, units[i][2], seq)
            code = jnp.where(u == i, units[i][3], code)
        return seq, code

    def w_copy(kv, layer, slot):
        return pltpu.make_async_copy((wk, wv)[kv].at[layer], wbuf.at[slot, kv], w_sem.at[slot, kv])

    def y_copy(u):
        s, i = units[u][:2]
        return pltpu.make_async_copy(srcs[s].at[i], ybuf.at[u], y_sem.at[u])

    def y_wait(u):
        pltpu.make_async_copy(srcs[0].at[0], ybuf.at[u], y_sem.at[u]).wait()

    def run(*accs):
        acc = [[[accs[(kv * 2 + q) * PIECES + p] for p in range(PIECES)] for q in range(2)] for kv in range(2)]

        def push(u, tile, reg):
            for q in range(2):
                pltpu.matmul_push_rhs(ybuf[u, pl.ds(q * 256, 256), pl.ds(tile * 256, 256)], staging_register=reg, mxu_index=q, transpose=True)

        def feed(kv, slot, tile, reg):
            for p in range(PIECES):
                lhs = wbuf[slot, kv, pl.ds(p * ROWS, ROWS), pl.ds(tile * 256, 256)]
                for q in range(2):
                    pltpu.matmul_acc_lhs(acc[kv][q][p], lhs, load_staged_rhs=reg if p == 0 else None)

        def drain(kv, p, slot):
            for q in range(2):
                obuf[kv, slot, pl.ds(p * ROWS, ROWS), pl.ds(q * 256, 256)] = pltpu.matmul_pop(acc[kv][q][p]).astype(jnp.bfloat16)

        w_copy(0, 0, 0).start()
        y_copy(0).start()
        w_copy(1, 0, 0).start()
        for u in range(1, n):
            y_copy(u).start()
        out_copy(0, 0, 0).start()
        out_copy(1, 0, 0).start()
        y_copy(0).wait()
        for kv in range(2):
            for p in range(PIECES):
                drain(kv, p, 1)
        push(0, 0, 1)
        for p in range(PIECES):
            for q in range(2):
                pltpu.matmul_acc_lhs(acc[1][q][p], jnp.zeros((ROWS, 256), jnp.bfloat16), load_staged_rhs=1 if p == 0 else None)
        push(0, 0, 0)

        def trip(layer, u, first):
            t = layer * n + u
            slot, oslot = layer % 2, t % 2
            out_copy(0, t - 2, 0).wait()
            out_copy(1, t - 3, 0).wait()
            out_copy(0, t - 1, 1 - oslot).start()
            out_copy(1, t - 2, oslot).start()
            if first:
                @pl.when(u + 1 < n)
                def _():
                    y_wait(u + 1)
            nxt = lax.rem(u + 1, n)
            for i in range(2 * NT):
                kv, tile = divmod(i, NT)
                feed(kv, slot, tile, i % 2)
                if i < 2 * NT - 1:
                    push(u, (i + 1) % NT, (i + 1) % 2)
                else:
                    push(nxt, 0, 0)
                if 1 <= tile <= PIECES:
                    drain(1 - kv, tile - 1, 1 - oslot if kv == 0 else oslot)

        for layer in range(1):
            for kv in range(2):
                w_copy(kv, 0, 0).wait()
            for kv in range(2):
                w_copy(kv, 1, 1).start()
        lax.fori_loop(0, n, lambda u, c: (trip(0, u, True), c)[1], 0)

        def layer_loop(layer, c):
            slot = layer % 2
            for kv in range(2):
                w_copy(kv, layer, slot).wait()
            nl = jnp.minimum(layer + 1, L - 1)
            for kv in range(2):
                w_copy(kv, nl, 1 - slot).start()
            lax.fori_loop(0, n, lambda u, c: (trip(layer, u, False), c)[1], 0)
            return c
        lax.fori_loop(1, L, layer_loop, 0)
        T = L * n
        for kv in range(2):
            w_copy(kv, L - 1, L % 2).wait()
        out_copy(0, T - 2, 0).wait()
        out_copy(1, T - 3, 0).wait()
        out_copy(0, T - 1, (T - 1) % 2).start()
        out_copy(1, T - 2, (T - 2) % 2).start()
        for p in range(PIECES):
            drain(1, p, (T - 1) % 2)
        out_copy(1, T - 2, 0).wait()
        out_copy(1, T - 1, (T - 1) % 2).start()
        out_copy(0, T - 1, 0).wait()
        out_copy(1, T - 1, 0).wait()
        for p in range(PIECES):
            for q in range(2):
                pltpu.matmul_acc_lhs(acc[0][q][p], jnp.zeros((ROWS, 256), jnp.bfloat16), load_staged_rhs=0 if p == 0 else None)

    pl.run_scoped(run, *[pltpu.ACC(q)((ROWS, 256), jnp.float32) for kv in range(2) for q in range(2) for p in range(PIECES)])

def project(sources, units, wk, wv, prev):
    n = len(units)
    out = jax.ShapeDtypeStruct((L, 6, HK, 4 * TOK), jnp.bfloat16)
    args = list(sources) + [wk, wv] + (list(prev) if prev else [])
    k = len(sources) + 2
    return pl.pallas_call(
        functools.partial(proj_body, units, len(sources), bool(prev)),
        out_shape=[out, out],
        in_specs=[pl.BlockSpec(memory_space=pl.ANY)] * len(args),
        out_specs=[pl.BlockSpec(memory_space=pl.ANY)] * 2,
        scratch_shapes=[
            pltpu.VMEM((n, TOK, D), jnp.bfloat16),
            pltpu.VMEM((2, 2, HK, D), jnp.bfloat16),
            pltpu.VMEM((2, 2, HK, TOK), jnp.bfloat16),
            pltpu.SemaphoreType.DMA((n,)),
            pltpu.SemaphoreType.DMA((2, 2)),
            pltpu.SemaphoreType.DMA((2,)),
        ],
        input_output_aliases={k: 0, k + 1: 1} if prev else {},
        cost_estimate=pl.CostEstimate(flops=2 * n * TOK * D * HK * 2 * L, bytes_accessed=n * (TOK * D * 2 + 2 * L * HK * TOK * 2) + 4 * L * HK * D, transcendentals=0),
        compiler_params=pltpu.CompilerParams(vmem_limit_bytes=48 * 1024 * 1024, has_side_effects=True),
    )(*args)


def PLAN(me, mt, fr, fw):
    return [me, mt + fr[:1], fw[:1] + fr[1:4], fw[1:4] + fr[4:5], fw[4:5] + fr[5:], fw[5:]]


def rms_norm(enc_out, norm_scale):
    acts = enc_out.astype(jnp.float32)
    mean_sq = jnp.mean(acts * acts, axis=-1, keepdims=True)
    return (acts * lax.rsqrt(mean_sq + NORM_EPS) * norm_scale.astype(jnp.float32)).astype(jnp.bfloat16)


def swap(x, code):
    return lax.ppermute(x, "tp", [(i, i ^ code) for i in range(4)])


def solution(mesh):
    def per_device(enc_out, norm_scale, w_key, w_value):
        wk = jnp.transpose(w_key, (0, 2, 3, 1)).reshape(L, HK, D)
        wv = jnp.transpose(w_value, (0, 2, 3, 1)).reshape(L, HK, D)
        y = [rms_norm(enc_out[c : c + 1], norm_scale) for c in range(6)]
        far = [swap(y[c], 2) for c in range(6)]
        mate = [swap(y[c], 1) for c in range(6)]
        fwd = [swap(far[c], 1) for c in range(6)]
        me, mt, fr, fw = [[[src[c], (c, code)] for c in range(6)] for src, code in ((y, 0), (mate, 1), (far, 2), (fwd, 3))]
        plan = PLAN(me, mt, fr, fw)
        out = None
        for group in plan:
            sources = [g[0] for g in group]
            units = [(i, 0, *g[1]) for i, g in enumerate(group)]
            out = project(sources, units, wk, wv, out)
        return tuple(jnp.transpose(o.reshape(L, 6, 8, 64, 4 * TOK), (0, 1, 4, 2, 3)) for o in out)

    weight_spec = P(None, None, "tp", None)
    cache_spec = P(None, "dp", None, "tp", None)
    return jax.shard_map(per_device, mesh=mesh, in_specs=(P("dp", "tp", None), P(None), weight_spec, weight_spec), out_specs=(cache_spec, cache_spec), check_vma=False)
```

time: 766 us -> 501 us (0.65)
  Pallas kernels: 0 us -> 351 us
  matrix products: 336 us -> 0 us
  waiting for transfers between devices: 298 us -> 126 us
  local copies, waits for them, and re-layouts: 98.8 us -> 2.99 us
  between operations: 14 us -> 0.98 us
  starting transfers between devices: 0.04 us -> 9.6 us
  other arithmetic: 19.5 us -> 10.1 us
    pallas_call x0 -> x6, Pallas kernels: none -> 351 us  [project(): pl.pallas_call(functools.partial(proj_body, units, len(sources), bool(pre...]
    dot_general x2 -> x0, matrix products: 336 us -> none  [the longest x1 168 us: per_device(): jnp.einsum('bsd,ldhk->lbshk', gathered, w_key, preferred_element_type=jnp...]
    all_gather x1 -> x0, waiting for transfers between devices: 297 us -> none  [per_device(): gathered = lax.all_gather(normed, 'tp', axis=1, tiled=True)]
    ppermute x0 -> x18, waiting for transfers between devices: none -> 126 us  [swap(): return lax.ppermute(x, 'tp', [(i, i ^ code) for i in range(4)])]
    unnamed x2 -> x14, local copies, waits for them, and re-layouts: 98.8 us -> 2.99 us
    ppermute x0 -> x18, starting transfers between devices: none -> 9.6 us  [swap(): return lax.ppermute(x, 'tp', [(i, i ^ code) for i in range(4)])]
    convert_element_type x1, other arithmetic: 11.7 us -> 4 us  [rms_norm(): (acts * lax.rsqrt(mean_sq + NORM_EPS) * norm_scale.astype(jnp.float32)).a...]
  transfers between devices with their start and end apart: 1 -> 18, of which waited for: 1 -> 3; matrix products, arithmetic and copies ran while one was open for 0% -> 0% of each run, Pallas kernels for 0% -> 66%
where the time goes in v1:
time: 501 us
  Pallas kernels  351 us (70%)
  waiting for transfers between devices  126 us (25%)
  other arithmetic  10.1 us (2%)
  starting transfers between devices  9.6 us (2%)
    pallas_call x6, Pallas kernels, project(): pl.pallas_call(functools.partial(proj_body, units, len(sources), bool(pre...  351 us
    ppermute x18, waiting for transfers between devices, swap(): return lax.ppermute(x, 'tp', [(i, i ^ code) for i in range(4)])  126 us
  transfers between devices with their start and end apart: 18, of which 3 were waited for; matrix products, arithmetic and copies ran while one was open for 0% of the time, Pallas kernels for 66%

profile of v1, /device:TPU:0, one launch (start us, length us, event | category | flops | bytes accessed | tf_op | source)
XLA Modules:
  0.0 500.7 jit_solution(13722847959496075506)
XLA Ops:
  0.6 6.0 %fusion.15 = (f32[512]{0:T(512)S(1)}, f32[512]{0:T(512)S(1)}, f32[512]{0:T(512)S(1)}, f32[512]{0:T(512)S(1)}, f32[512]{0:T(512)S(1)}, /*index=5*/f32[512]{0:T(512)S(1)}) fusion(bf16[6,512,2048]{2,1,0:T(8,128)(2,1)} %param.4), kind=kLoop, calls=%fused_computation.27 | loop fusion | flops 18871296 | bytes 12595200 | tf_op jit(solution)/shard_map/reduce_sum | solution.py:169
  6.8 2.1 copy-done
  8.9 4.0 fusion.17
  12.9 3.3 collective-permute-start.10
  16.2 0.5 collective-permute-start.13
  16.8 45.9 %collective-permute-done.10.refs_6_ = bf16[1,512,2048]{2,1,0:T(8,128)(2,1)S(1)} collective-permute-done((bf16[1,512,2048]{2,1,0:T(8,128)(2,1)S(1)}, bf16[1,512,2048]{2,1,0:T(8,128)(2,1)S(1)}, u32[]{:S(2)}, u32[]{:S(2)}) %collective-permute-start.10) | collective-permute-done | bytes 2097184 | tf_op jit(solution)/shard_map/ppermute | solution.py:174
  62.7 0.5 collective-permute-start.16
  63.2 0.8 copy-done.4
  64.1 84.2 %shard_map.59 = (bf16[6,6,512,2048]{3,2,1,0:T(8,128)(2,1)}, bf16[6,6,512,2048]{3,2,1,0:T(8,128)(2,1)}) custom-call(bf16[1,512,2048]{2,1,0:T(8,128)(2,1)S(1)} %get-tuple-element.32.refs_0_, bf16[1,512,2048]{2,1,0:T(8,128)(2,1)S(1)} %get-tuple-element.34.refs_1_, bf16[1,512,2048]{2,1,0:T(8,128)(2,1)} %get-tuple-element.35.refs_2_, ...), custom_call_target="tpu_custom_call" | custom-call | flops 77309411328 | bytes 75497472 | tf_op jit(solution)/shard_map/pallas_call | solution.py:144
  148.3 2.1 collective-permute-start.6
  150.4 0.0 collective-permute-start.8
  150.5 2.0 collective-permute-start.2
  152.4 0.0 collective-permute-start
  152.5 98.0 %shard_map.60 = (bf16[6,6,512,2048]{3,2,1,0:T(8,128)(2,1)}, bf16[6,6,512,2048]{3,2,1,0:T(8,128)(2,1)}) custom-call(bf16[1,512,2048]{2,1,0:T(8,128)(2,1)S(1)} %collective-permute-done.12.refs_0_, bf16[1,512,2048]{2,1,0:T(8,128)(2,1)S(1)} %collective-permute-done.13.refs_1_, ...), custom_call_target="tpu_custom_call", output_to_operand_aliasing={{0}: (9, {}), {1}: (10, {})} | custom-call | flops 90194313216 | bytes 83886080 | tf_op jit(solution)/shard_map/pallas_call | solution.py:144
  250.5 0.5 collective-permute-start.5
  251.0 0.0 collective-permute-start.7
  251.1 35.7 %collective-permute-done.2.refs_3_ = bf16[1,512,2048]{2,1,0:T(8,128)(2,1)S(1)} collective-permute-done((bf16[1,512,2048]{2,1,0:T(8,128)(2,1)}, bf16[1,512,2048]{2,1,0:T(8,128)(2,1)S(1)}, u32[]{:S(2)}, u32[]{:S(2)}) %collective-permute-start.2) | collective-permute-done | bytes 2097184 | tf_op jit(solution)/shard_map/ppermute | solution.py:174
  286.8 44.7 %collective-permute-done.refs_1_ = bf16[1,512,2048]{2,1,0:T(8,128)(2,1)} collective-permute-done((bf16[1,512,2048]{2,1,0:T(8,128)(2,1)}, bf16[1,512,2048]{2,1,0:T(8,128)(2,1)}, u32[]{:S(2)}, u32[]{:S(2)}) %collective-permute-start) | collective-permute-done | bytes 2097184 | tf_op jit(solution)/shard_map/ppermute | solution.py:174
  331.5 0.0 collective-permute-start.3
  331.6 0.5 collective-permute-start.1
  332.0 58.1 %shard_map.61 = (bf16[6,6,512,2048]{3,2,1,0:T(8,128)(2,1)}, bf16[6,6,512,2048]{3,2,1,0:T(8,128)(2,1)}) custom-call(bf16[1,512,2048]{2,1,0:T(8,128)(2,1)S(1)} %collective-permute-done.11.refs_0_, bf16[1,512,2048]{2,1,0:T(8,128)(2,1)S(1)} %collective-permute-done.4.refs_1_, ...), custom_call_target="tpu_custom_call", output_to_operand_aliasing={{0}: (6, {}), {1}: (7, {})} | custom-call | flops 51539607552 | bytes 58720256 | tf_op jit(solution)/shard_map/pallas_call | solution.py:144
  390.2 57.9 %shard_map.62 = (bf16[6,6,512,2048]{3,2,1,0:T(8,128)(2,1)}, bf16[6,6,512,2048]{3,2,1,0:T(8,128)(2,1)}) custom-call(bf16[1,512,2048]{2,1,0:T(8,128)(2,1)S(1)} %collective-permute-done.5.refs_0_, bf16[1,512,2048]{2,1,0:T(8,128)(2,1)S(1)} %collective-permute-done.7.refs_1_, ...), custom_call_target="tpu_custom_call", output_to_operand_aliasing={{0}: (6, {}), {1}: (7, {})} | custom-call | flops 51539607552 | bytes 58720256 | tf_op jit(solution)/shard_map/pallas_call | solution.py:144
  448.0 31.7 %shard_map.63 = (bf16[6,6,512,2048]{3,2,1,0:T(8,128)(2,1)}, bf16[6,6,512,2048]{3,2,1,0:T(8,128)(2,1)}) custom-call(bf16[1,512,2048]{2,1,0:T(8,128)(2,1)S(1)} %collective-permute-done.3.refs_0_, bf16[1,512,2048]{2,1,0:T(8,128)(2,1)} %collective-permute-done.refs_1_, bf16[6,512,2048]{2,1,0:T(8,128)(2,1)} %bitcast.16, ...), custom_call_target="tpu_custom_call", output_to_operand_aliasing={{0}: (4, {}), {1}: (5, {})} | custom-call | flops 25769803776 | bytes 41943040 | tf_op jit(solution)/shard_map/pallas_call | solution.py:144
  479.8 20.8 %shard_map.64 = (bf16[6,6,512,2048]{3,2,1,0:T(8,128)(2,1)}, bf16[6,6,512,2048]{3,2,1,0:T(8,128)(2,1)}) custom-call(bf16[1,512,2048]{2,1,0:T(8,128)(2,1)} %collective-permute-done.1.refs_0_, bf16[6,512,2048]{2,1,0:T(8,128)(2,1)} %bitcast.17, bf16[6,512,2048]{2,1,0:T(8,128)(2,1)} %bitcast.23, ...), custom_call_target="tpu_custom_call", output_to_operand_aliasing={{0}: (3, {}), {1}: (4, {})} | custom-call | flops 12884901888 | bytes 33554432 | tf_op jit(solution)/shard_map/pallas_call | solution.py:144
  (38 shorter events, 0.1 us)
Async XLA Ops:
  0.6 8.3 %copy-start = (bf16[6,512,2048]{2,1,0:T(8,128)(2,1)S(1)}, bf16[6,512,2048]{2,1,0:T(8,128)(2,1)}, u32[]{:S(2)}) copy-start(bf16[6,512,2048]{2,1,0:T(8,128)(2,1)} %param.4) | copy-start | bytes 37748740
  0.6 6.1 %copy-start.3 = (bf16[2048]{0:T(1024)(128)(2,1)S(1)}, bf16[2048]{0:T(1024)(128)(2,1)}, u32[]{:S(2)}) copy-start(bf16[2048]{0:T(1024)(128)(2,1)} %param.5) | copy-start | bytes 12292
  12.9 51.2 %copy-start.1 = (bf16[1,512,2048]{2,1,0:T(8,128)(2,1)}, bf16[1,512,2048]{2,1,0:T(8,128)(2,1)S(1)}, u32[]{:S(2)}) copy-start(bf16[1,512,2048]{2,1,0:T(8,128)(2,1)S(1)} %get-tuple-element.37.refs_5_) | copy-start | bytes 6291460
  12.9 51.2 %copy-start.2 = (bf16[1,512,2048]{2,1,0:T(8,128)(2,1)}, bf16[1,512,2048]{2,1,0:T(8,128)(2,1)S(1)}, u32[]{:S(2)}) copy-start(bf16[1,512,2048]{2,1,0:T(8,128)(2,1)S(1)} %get-tuple-element.33.refs_4_) | copy-start | bytes 6291460
  12.9 49.8 %collective-permute-start.10 = (bf16[1,512,2048]{2,1,0:T(8,128)(2,1)S(1)}, bf16[1,512,2048]{2,1,0:T(8,128)(2,1)S(1)}, u32[]{:S(2)}, u32[]{:S(2)}) collective-permute-start(bf16[1,512,2048]{2,1,0:T(8,128)(2,1)S(1)} %get-tuple-element.32.refs_0_), channel_id=1, source_target_pairs={{0,2},{1,3},{2,0},{3,1},{4,6},{5,7},{6,4},{7,5}} | collective-permute-start | bytes 6291464 | tf_op jit(solution)/shard_map/ppermute | solution.py:174
  16.2 46.5 %collective-permute-start.12 = (bf16[1,512,2048]{2,1,0:T(8,128)(2,1)S(1)}, bf16[1,512,2048]{2,1,0:T(8,128)(2,1)S(1)}, u32[]{:S(2)}, u32[]{:S(2)}) collective-permute-start(bf16[1,512,2048]{2,1,0:T(8,128)(2,1)S(1)} %get-tuple-element.32.refs_0_), channel_id=1, source_target_pairs={{0,1},{1,0},{2,3},{3,2},{4,5},{5,4},{6,7},{7,6}} | collective-permute-start | bytes 6291464 | tf_op jit(solution)/shard_map/ppermute | solution.py:174
  16.2 47.0 %collective-permute-start.13 = (bf16[1,512,2048]{2,1,0:T(8,128)(2,1)S(1)}, bf16[1,512,2048]{2,1,0:T(8,128)(2,1)S(1)}, u32[]{:S(2)}, u32[]{:S(2)}) collective-permute-start(bf16[1,512,2048]{2,1,0:T(8,128)(2,1)S(1)} %get-tuple-element.34.refs_1_), channel_id=1, source_target_pairs={{0,1},{1,0},{2,3},{3,2},{4,5},{5,4},{6,7},{7,6}} | collective-permute-start | bytes 6291464 | tf_op jit(solution)/shard_map/ppermute | solution.py:174
  16.7 135.7 %collective-permute-start.4 = (bf16[1,512,2048]{2,1,0:T(8,128)(2,1)S(1)}, bf16[1,512,2048]{2,1,0:T(8,128)(2,1)S(1)}, u32[]{:S(2)}, u32[]{:S(2)}) collective-permute-start(bf16[1,512,2048]{2,1,0:T(8,128)(2,1)S(1)} %get-tuple-element.34.refs_1_), channel_id=1, source_target_pairs={{0,2},{1,3},{2,0},{3,1},{4,6},{5,7},{6,4},{7,5}} | collective-permute-start | bytes 6291464 | tf_op jit(solution)/shard_map/ppermute | solution.py:174
  16.8 131.6 %collective-permute-start.14 = (bf16[1,512,2048]{2,1,0:T(8,128)(2,1)}, bf16[1,512,2048]{2,1,0:T(8,128)(2,1)}, u32[]{:S(2)}, u32[]{:S(2)}) collective-permute-start(bf16[1,512,2048]{2,1,0:T(8,128)(2,1)} %get-tuple-element.35.refs_2_), channel_id=1, source_target_pairs={{0,1},{1,0},{2,3},{3,2},{4,5},{5,4},{6,7},{7,6}} | collective-permute-start | bytes 6291464 | tf_op jit(solution)/shard_map/ppermute | solution.py:174
  62.7 87.7 %collective-permute-start.15 = (bf16[1,512,2048]{2,1,0:T(8,128)(2,1)}, bf16[1,512,2048]{2,1,0:T(8,128)(2,1)}, u32[]{:S(2)}, u32[]{:S(2)}) collective-permute-start(bf16[1,512,2048]{2,1,0:T(8,128)(2,1)} %get-tuple-element.36.refs_3_), channel_id=1, source_target_pairs={{0,1},{1,0},{2,3},{3,2},{4,5},{5,4},{6,7},{7,6}} | collective-permute-start | bytes 6291464 | tf_op jit(solution)/shard_map/ppermute | solution.py:174
  62.7 87.7 %collective-permute-start.16 = (bf16[1,512,2048]{2,1,0:T(8,128)(2,1)S(1)}, bf16[1,512,2048]{2,1,0:T(8,128)(2,1)}, u32[]{:S(2)}, u32[]{:S(2)}) collective-permute-start(bf16[1,512,2048]{2,1,0:T(8,128)(2,1)S(1)} %get-tuple-element.33.refs_4_), channel_id=1, source_target_pairs={{0,1},{1,0},{2,3},{3,2},{4,5},{5,4},{6,7},{7,6}} | collective-permute-start | bytes 6291464 | tf_op jit(solution)/shard_map/ppermute | solution.py:174
  64.1 88.4 %collective-permute-start.17 = (bf16[1,512,2048]{2,1,0:T(8,128)(2,1)S(1)}, bf16[1,512,2048]{2,1,0:T(8,128)(2,1)}, u32[]{:S(2)}, u32[]{:S(2)}) collective-permute-start(bf16[1,512,2048]{2,1,0:T(8,128)(2,1)S(1)} %get-tuple-element.37.refs_5_), channel_id=1, source_target_pairs={{0,1},{1,0},{2,3},{3,2},{4,5},{5,4},{6,7},{7,6}} | collective-permute-start | bytes 6291464 | tf_op jit(solution)/shard_map/ppermute | solution.py:174
  148.3 102.1 %collective-permute-start.6 = (bf16[1,512,2048]{2,1,0:T(8,128)(2,1)}, bf16[1,512,2048]{2,1,0:T(8,128)(2,1)S(1)}, u32[]{:S(2)}, u32[]{:S(2)}) collective-permute-start(bf16[1,512,2048]{2,1,0:T(8,128)(2,1)} %get-tuple-element.35.refs_2_), channel_id=1, source_target_pairs={{0,2},{1,3},{2,0},{3,1},{4,6},{5,7},{6,4},{7,5}} | collective-permute-start | bytes 6291464 | tf_op jit(solution)/shard_map/ppermute | solution.py:174
  150.4 100.6 %collective-permute-start.8 = (bf16[1,512,2048]{2,1,0:T(8,128)(2,1)}, bf16[1,512,2048]{2,1,0:T(8,128)(2,1)}, u32[]{:S(2)}, u32[]{:S(2)}) collective-permute-start(bf16[1,512,2048]{2,1,0:T(8,128)(2,1)} %get-tuple-element.36.refs_3_), channel_id=1, source_target_pairs={{0,2},{1,3},{2,0},{3,1},{4,6},{5,7},{6,4},{7,5}} | collective-permute-start | bytes 6291464 | tf_op jit(solution)/shard_map/ppermute | solution.py:174
  150.5 136.3 %collective-permute-start.2 = (bf16[1,512,2048]{2,1,0:T(8,128)(2,1)}, bf16[1,512,2048]{2,1,0:T(8,128)(2,1)S(1)}, u32[]{:S(2)}, u32[]{:S(2)}) collective-permute-start(bf16[1,512,2048]{2,1,0:T(8,128)(2,1)} %copy-done.2), channel_id=1, source_target_pairs={{0,2},{1,3},{2,0},{3,1},{4,6},{5,7},{6,4},{7,5}} | collective-permute-start | bytes 6291464 | tf_op jit(solution)/shard_map/ppermute | solution.py:174
  152.4 179.1 %collective-permute-start = (bf16[1,512,2048]{2,1,0:T(8,128)(2,1)}, bf16[1,512,2048]{2,1,0:T(8,128)(2,1)}, u32[]{:S(2)}, u32[]{:S(2)}) collective-permute-start(bf16[1,512,2048]{2,1,0:T(8,128)(2,1)} %copy-done.1), channel_id=1, source_target_pairs={{0,2},{1,3},{2,0},{3,1},{4,6},{5,7},{6,4},{7,5}} | collective-permute-start | bytes 6291464 | tf_op jit(solution)/shard_map/ppermute | solution.py:174
  152.5 179.1 %collective-permute-start.11 = (bf16[1,512,2048]{2,1,0:T(8,128)(2,1)}, bf16[1,512,2048]{2,1,0:T(8,128)(2,1)S(1)}, u32[]{:S(2)}, u32[]{:S(2)}) collective-permute-start(bf16[1,512,2048]{2,1,0:T(8,128)(2,1)} %copy-done.4), channel_id=1, source_target_pairs={{0,1},{1,0},{2,3},{3,2},{4,5},{5,4},{6,7},{7,6}} | collective-permute-start | bytes 6291464 | tf_op jit(solution)/shard_map/ppermute | solution.py:174
  250.5 81.6 %copy-start.6 = (bf16[1,512,2048]{2,1,0:T(8,128)(2,1)}, bf16[1,512,2048]{2,1,0:T(8,128)(2,1)S(1)}, u32[]{:S(2)}) copy-start(bf16[1,512,2048]{2,1,0:T(8,128)(2,1)S(1)} %collective-permute-done.6.refs_2_) | copy-start | bytes 6291460
  250.5 139.6 %collective-permute-start.5 = (bf16[1,512,2048]{2,1,0:T(8,128)(2,1)S(1)}, bf16[1,512,2048]{2,1,0:T(8,128)(2,1)S(1)}, u32[]{:S(2)}, u32[]{:S(2)}) collective-permute-start(bf16[1,512,2048]{2,1,0:T(8,128)(2,1)S(1)} %collective-permute-done.4.refs_1_), channel_id=1, source_target_pairs={{0,1},{1,0},{2,3},{3,2},{4,5},{5,4},{6,7},{7,6}} | collective-permute-start | bytes 6291464 | tf_op jit(solution)/shard_map/ppermute | solution.py:174
  251.0 139.1 %collective-permute-start.7 = (bf16[1,512,2048]{2,1,0:T(8,128)(2,1)S(1)}, bf16[1,512,2048]{2,1,0:T(8,128)(2,1)S(1)}, u32[]{:S(2)}, u32[]{:S(2)}) collective-permute-start(bf16[1,512,2048]{2,1,0:T(8,128)(2,1)S(1)} %collective-permute-done.6.refs_2_), channel_id=1, source_target_pairs={{0,1},{1,0},{2,3},{3,2},{4,5},{5,4},{6,7},{7,6}} | collective-permute-start | bytes 6291464 | tf_op jit(solution)/shard_map/ppermute | solution.py:174
  286.8 103.3 %copy-start.5 = (bf16[1,512,2048]{2,1,0:T(8,128)(2,1)}, bf16[1,512,2048]{2,1,0:T(8,128)(2,1)S(1)}, u32[]{:S(2)}) copy-start(bf16[1,512,2048]{2,1,0:T(8,128)(2,1)S(1)} %collective-permute-done.2.refs_3_) | copy-start | bytes 6291460
  286.8 103.4 %collective-permute-start.9 = (bf16[1,512,2048]{2,1,0:T(8,128)(2,1)}, bf16[1,512,2048]{2,1,0:T(8,128)(2,1)}, u32[]{:S(2)}, u32[]{:S(2)}) collective-permute-start(bf16[1,512,2048]{2,1,0:T(8,128)(2,1)} %collective-permute-done.8.refs_3_), channel_id=1, source_target_pairs={{0,1},{1,0},{2,3},{3,2},{4,5},{5,4},{6,7},{7,6}} | collective-permute-start | bytes 6291464 | tf_op jit(solution)/shard_map/ppermute | solution.py:174
  331.5 116.5 %collective-permute-start.3 = (bf16[1,512,2048]{2,1,0:T(8,128)(2,1)S(1)}, bf16[1,512,2048]{2,1,0:T(8,128)(2,1)S(1)}, u32[]{:S(2)}, u32[]{:S(2)}) collective-permute-start(bf16[1,512,2048]{2,1,0:T(8,128)(2,1)S(1)} %collective-permute-done.2.refs_3_), channel_id=1, source_target_pairs={{0,1},{1,0},{2,3},{3,2},{4,5},{5,4},{6,7},{7,6}} | collective-permute-start | bytes 6291464 | tf_op jit(solution)/shard_map/ppermute | solution.py:174
  331.6 148.2 %collective-permute-start.1 = (bf16[1,512,2048]{2,1,0:T(8,128)(2,1)}, bf16[1,512,2048]{2,1,0:T(8,128)(2,1)}, u32[]{:S(2)}, u32[]{:S(2)}) collective-permute-start(bf16[1,512,2048]{2,1,0:T(8,128)(2,1)} %collective-permute-done.refs_1_), channel_id=1, source_target_pairs={{0,1},{1,0},{2,3},{3,2},{4,5},{5,4},{6,7},{7,6}} | collective-permute-start | bytes 6291464 | tf_op jit(solution)/shard_map/ppermute | solution.py:174
  (1 other events, 1.4 us)

commit v2 on v1

--- a/solution.py
+++ b/solution.py
@@ -10,6 +10,7 @@
 L, D, HK, TOK = 6, 2048, 512, 512
 PIECES, ROWS = 4, 128
 NT = D // 256
+
 
 def proj_body(units, n_src, has_prev, *refs):
     n = len(units)
@@ -100,7 +101,7 @@
                 if 1 <= tile <= PIECES:
                     drain(1 - kv, tile - 1, 1 - oslot if kv == 0 else oslot)
 
-        for layer in range(1):
+        for _ in range(1):
             for kv in range(2):
                 w_copy(kv, 0, 0).wait()
             for kv in range(2):
@@ -116,6 +117,7 @@
                 w_copy(kv, nl, 1 - slot).start()
             lax.fori_loop(0, n, lambda u, c: (trip(layer, u, False), c)[1], 0)
             return c
+
         lax.fori_loop(1, L, layer_loop, 0)
         T = L * n
         for kv in range(2):
@@ -134,7 +136,8 @@
             for q in range(2):
                 pltpu.matmul_acc_lhs(acc[0][q][p], jnp.zeros((ROWS, 256), jnp.bfloat16), load_staged_rhs=0 if p == 0 else None)
 
-    pl.run_scoped(run, *[pltpu.ACC(q)((ROWS, 256), jnp.float32) for kv in range(2) for q in range(2) for p in range(PIECES)])
+    pl.run_scoped(run, *[pltpu.ACC(q)((ROWS, 256), jnp.float32) for _ in range(2) for q in range(2) for _ in range(PIECES)])
+
 
 def project(sources, units, wk, wv, prev):
     n = len(units)
@@ -156,12 +159,22 @@
         ],
         input_output_aliases={k: 0, k + 1: 1} if prev else {},
         cost_estimate=pl.CostEstimate(flops=2 * n * TOK * D * HK * 2 * L, bytes_accessed=n * (TOK * D * 2 + 2 * L * HK * TOK * 2) + 4 * L * HK * D, transcendentals=0),
-        compiler_params=pltpu.CompilerParams(vmem_limit_bytes=48 * 1024 * 1024, has_side_effects=True),
+        compiler_params=pltpu.CompilerParams(vmem_limit_bytes=60 * 1024 * 1024, has_side_effects=True),
     )(*args)
 
 
-def PLAN(me, mt, fr, fw):
-    return [me, mt + fr[:1], fw[:1] + fr[1:4], fw[1:4] + fr[4:5], fw[4:5] + fr[5:], fw[5:]]
+def units_of(name, *chunks):
+    return [(name, c) for c in chunks]
+
+
+PLAN = [
+    (units_of("own", *range(6)), (0,)),
+    (units_of("mate", *range(6)) + units_of("far", 0), (1, 2, 3)),
+    (units_of("fwd", 0) + units_of("far", 1, 2, 3), (4,)),
+    (units_of("fwd", 1, 2, 3) + units_of("far", 4), (5,)),
+    (units_of("fwd", 4) + units_of("far", 5), ()),
+    (units_of("fwd", 5), ()),
+]
 
 
 def rms_norm(enc_out, norm_scale):
@@ -175,22 +188,27 @@
 
 
 def solution(mesh):
-    def per_device(enc_out, norm_scale, w_key, w_value):
+    def gather_and_project(enc_out, norm_scale, w_key, w_value):
         wk = jnp.transpose(w_key, (0, 2, 3, 1)).reshape(L, HK, D)
         wv = jnp.transpose(w_value, (0, 2, 3, 1)).reshape(L, HK, D)
         y = [rms_norm(enc_out[c : c + 1], norm_scale) for c in range(6)]
         far = [swap(y[c], 2) for c in range(6)]
         mate = [swap(y[c], 1) for c in range(6)]
-        fwd = [swap(far[c], 1) for c in range(6)]
-        me, mt, fr, fw = [[[src[c], (c, code)] for c in range(6)] for src, code in ((y, 0), (mate, 1), (far, 2), (fwd, 3))]
-        plan = PLAN(me, mt, fr, fw)
+        fwd = [None] * 6
+        kept = {"own": y, "mate": mate, "far": far, "fwd": fwd}
+        code = {"own": 0, "mate": 1, "far": 2, "fwd": 3}
         out = None
-        for group in plan:
-            sources = [g[0] for g in group]
-            units = [(i, 0, *g[1]) for i, g in enumerate(group)]
+        for group, forward in PLAN:
+            sources = [kept[name][c] for name, c in group]
+            units = [(i, 0, c, code[name]) for i, (name, c) in enumerate(group)]
             out = project(sources, units, wk, wv, out)
+            if forward:
+                out, moved = lax.optimization_barrier((out, [far[c] for c in forward]))
+                for c, block in zip(forward, moved):
+                    far[c] = block
+                    fwd[c] = swap(block, 1)
         return tuple(jnp.transpose(o.reshape(L, 6, 8, 64, 4 * TOK), (0, 1, 4, 2, 3)) for o in out)
 
     weight_spec = P(None, None, "tp", None)
     cache_spec = P(None, "dp", None, "tp", None)
-    return jax.shard_map(per_device, mesh=mesh, in_specs=(P("dp", "tp", None), P(None), weight_spec, weight_spec), out_specs=(cache_spec, cache_spec), check_vma=False)
+    return jax.shard_map(gather_and_project, mesh=mesh, in_specs=(P("dp", "tp", None), P(None), weight_spec, weight_spec), out_specs=(cache_spec, cache_spec), check_vma=False)

time: 501 us -> 513 us (1.024)
  Pallas kernels: 351 us -> 361 us
  waiting for transfers between devices: 126 us -> 120 us
    pallas_call x6, Pallas kernels: 351 us -> 361 us  [project(): pl.pallas_call(functools.partial(proj_body, units, len(sources), bool(pre...]
    ppermute x18, waiting for transfers between devices: 126 us -> 120 us  [swap(): return lax.ppermute(x, 'tp', [(i, i ^ code) for i in range(4)])]
  transfers between devices with their start and end apart: 18 -> 18, of which waited for: 3 -> 4; matrix products, arithmetic and copies ran while one was open for 0% -> 0% of each run, Pallas kernels for 66% -> 66%
where the time goes in v2:
time: 513 us
  Pallas kernels  361 us (70%)
  waiting for transfers between devices  120 us (23%)
  other arithmetic  12.6 us (2%)
  starting transfers between devices  11.3 us (2%)
  local copies, waits for them, and re-layouts  6.16 us (1%)
    pallas_call x6, Pallas kernels, project(): pl.pallas_call(functools.partial(proj_body, units, len(sources), bool(pre...  361 us
    ppermute x18, waiting for transfers between devices, swap(): return lax.ppermute(x, 'tp', [(i, i ^ code) for i in range(4)])  120 us
    ppermute x18, starting transfers between devices, swap(): return lax.ppermute(x, 'tp', [(i, i ^ code) for i in range(4)])  11.3 us
  transfers between devices with their start and end apart: 18, of which 4 were waited for; matrix products, arithmetic and copies ran while one was open for 0% of the time, Pallas kernels for 66%

profile of v2, /device:TPU:0, one launch (start us, length us, event | category | flops | bytes accessed | tf_op | source)
XLA Modules:
  0.0 512.9 jit_solution(538891299667349065)
XLA Ops:
  0.6 0.7 convert_element_type.45
  1.3 6.0 %fusion.15 = (f32[512]{0:T(512)S(1)}, f32[512]{0:T(512)S(1)}, f32[512]{0:T(512)S(1)}, f32[512]{0:T(512)S(1)}, f32[512]{0:T(512)S(1)}, /*index=5*/f32[512]{0:T(512)S(1)}) fusion(bf16[6,512,2048]{2,1,0:T(8,128)(2,1)} %param.4), kind=kLoop, calls=%fused_computation.27 | loop fusion | flops 18871296 | bytes 12595200 | tf_op jit(solution)/shard_map/reduce_sum | solution.py:182
  7.4 2.1 copy-done
  9.6 5.8 %fusion.17 = (bf16[1,512,2048]{2,1,0:T(8,128)(2,1)S(1)}, bf16[1,512,2048]{2,1,0:T(8,128)(2,1)}, bf16[1,512,2048]{2,1,0:T(8,128)(2,1)}, bf16[1,512,2048]{2,1,0:T(...) fusion(f32[512]{0:T(512)S(1)} %get-tuple-element.66, f32[2048]{0:T(1024)S(1)} %convert_element_type.45, ...), kind=kLoop, calls=%fused_computation.29 | loop fusion | flops 25165824 | bytes 25186304 | tf_op jit(solution)/shard_map/convert_element_type | solution.py:183
  15.4 0.8 collective-permute-start.5
  16.2 2.5 collective-permute-start.6
  19.4 0.6 collective-permute-done.5.refs_5_
  20.0 1.3 copy-done.3
  21.7 43.6 %collective-permute-done.6.refs_6_ = bf16[1,512,2048]{2,1,0:T(8,128)(2,1)} collective-permute-done((bf16[1,512,2048]{2,1,0:T(8,128)(2,1)}, bf16[1,512,2048]{2,1,0:T(8,128)(2,1)}, u32[]{:S(2)}, u32[]{:S(2)}) %collective-permute-start.6) | collective-permute-done | bytes 2097184 | tf_op jit(solution)/shard_map/ppermute | solution.py:187
  65.3 87.2 %shard_map.59 = (bf16[6,6,512,2048]{3,2,1,0:T(8,128)(2,1)}, bf16[6,6,512,2048]{3,2,1,0:T(8,128)(2,1)}) custom-call(bf16[1,512,2048]{2,1,0:T(8,128)(2,1)} %get-tuple-element.65.refs_0_, bf16[1,512,2048]{2,1,0:T(8,128)(2,1)} %get-tuple-element.61.refs_1_, bf16[1,512,2048]{2,1,0:T(8,128)(2,1)} %get-tuple-element.62.refs_2_, ...), custom_call_target="tpu_custom_call" | custom-call | flops 77309411328 | bytes 75497472 | tf_op jit(solution)/shard_map/pallas_call | solution.py:147
  152.6 1.7 collective-permute-start.15
  154.6 1.7 collective-permute-start.8
  156.7 101.6 %shard_map.60 = (bf16[6,6,512,2048]{3,2,1,0:T(8,128)(2,1)}, bf16[6,6,512,2048]{3,2,1,0:T(8,128)(2,1)}) custom-call(bf16[1,512,2048]{2,1,0:T(8,128)(2,1)} %collective-permute-done.refs_0_, bf16[1,512,2048]{2,1,0:T(8,128)(2,1)} %collective-permute-done.1.refs_1_, ...), custom_call_target="tpu_custom_call", output_to_operand_aliasing={{0}: (9, {}), {1}: (10, {})} | custom-call | flops 90194313216 | bytes 83886080 | tf_op jit(solution)/shard_map/pallas_call | solution.py:147
  258.2 1.8 collective-permute-start.14
  260.0 31.3 %collective-permute-done.8.refs_2_ = bf16[1,512,2048]{2,1,0:T(8,128)(2,1)} collective-permute-done((bf16[1,512,2048]{2,1,0:T(8,128)(2,1)}, bf16[1,512,2048]{2,1,0:T(8,128)(2,1)}, u32[]{:S(2)}, u32[]{:S(2)}) %collective-permute-start.8) | collective-permute-done | bytes 2097184 | tf_op jit(solution)/shard_map/ppermute | solution.py:187
  291.3 44.9 %collective-permute-done.9.refs_3_ = bf16[1,512,2048]{2,1,0:T(8,128)(2,1)} collective-permute-done((bf16[1,512,2048]{2,1,0:T(8,128)(2,1)}, bf16[1,512,2048]{2,1,0:T(8,128)(2,1)}, u32[]{:S(2)}, u32[]{:S(2)}) %collective-permute-start.9) | collective-permute-done | bytes 2097184 | tf_op jit(solution)/shard_map/ppermute | solution.py:187
  336.2 0.5 collective-permute-start.11
  336.7 59.9 %shard_map.61 = (bf16[6,6,512,2048]{3,2,1,0:T(8,128)(2,1)}, bf16[6,6,512,2048]{3,2,1,0:T(8,128)(2,1)}) custom-call(bf16[1,512,2048]{2,1,0:T(8,128)(2,1)} %collective-permute-done.13.refs_0_, bf16[1,512,2048]{2,1,0:T(8,128)(2,1)} %collective-permute-done.7.refs_1_, ...), custom_call_target="tpu_custom_call", output_to_operand_aliasing={{0}: (6, {}), {1}: (7, {})} | custom-call | flops 51539607552 | bytes 58720256 | tf_op jit(solution)/shard_map/pallas_call | solution.py:147
  396.7 1.3 copy-done.4
  398.0 0.5 collective-permute-start.17
  398.5 59.7 %shard_map.62 = (bf16[6,6,512,2048]{3,2,1,0:T(8,128)(2,1)}, bf16[6,6,512,2048]{3,2,1,0:T(8,128)(2,1)}) custom-call(bf16[1,512,2048]{2,1,0:T(8,128)(2,1)} %collective-permute-done.10.refs_0_, bf16[1,512,2048]{2,1,0:T(8,128)(2,1)} %collective-permute-done.11.refs_1_, ...), custom_call_target="tpu_custom_call", output_to_operand_aliasing={{0}: (6, {}), {1}: (7, {})} | custom-call | flops 51539607552 | bytes 58720256 | tf_op jit(solution)/shard_map/pallas_call | solution.py:147
  458.3 1.3 copy-done.1
  459.6 32.3 %shard_map.63 = (bf16[6,6,512,2048]{3,2,1,0:T(8,128)(2,1)}, bf16[6,6,512,2048]{3,2,1,0:T(8,128)(2,1)}) custom-call(bf16[1,512,2048]{2,1,0:T(8,128)(2,1)} %copy-done.1, bf16[1,512,2048]{2,1,0:T(8,128)(2,1)} %collective-permute-done.15.refs_1_, bf16[6,512,2048]{2,1,0:T(8,128)(2,1)} %bitcast.16, ...), custom_call_target="tpu_custom_call", output_to_operand_aliasing={{0}: (4, {}), {1}: (5, {})} | custom-call | flops 25769803776 | bytes 41943040 | tf_op jit(solution)/shard_map/pallas_call | solution.py:147
  492.0 20.8 %shard_map.64 = (bf16[6,6,512,2048]{3,2,1,0:T(8,128)(2,1)}, bf16[6,6,512,2048]{3,2,1,0:T(8,128)(2,1)}) custom-call(bf16[1,512,2048]{2,1,0:T(8,128)(2,1)} %collective-permute-done.16.refs_0_, bf16[6,512,2048]{2,1,0:T(8,128)(2,1)} %bitcast.17, bf16[6,512,2048]{2,1,0:T(8,128)(2,1)} %bitcast.23, ...), custom_call_target="tpu_custom_call", output_to_operand_aliasing={{0}: (3, {}), {1}: (4, {})} | custom-call | flops 12884901888 | bytes 33554432 | tf_op jit(solution)/shard_map/pallas_call | solution.py:147
  (34 shorter events, 1.8 us)
Async XLA Ops:
  1.3 8.2 %copy-start = (bf16[6,512,2048]{2,1,0:T(8,128)(2,1)S(1)}, bf16[6,512,2048]{2,1,0:T(8,128)(2,1)}, u32[]{:S(2)}) copy-start(bf16[6,512,2048]{2,1,0:T(8,128)(2,1)} %param.4) | copy-start | bytes 37748740
  15.4 49.9 %copy-start.2 = (bf16[1,512,2048]{2,1,0:T(8,128)(2,1)}, bf16[1,512,2048]{2,1,0:T(8,128)(2,1)S(1)}, u32[]{:S(2)}) copy-start(bf16[1,512,2048]{2,1,0:T(8,128)(2,1)S(1)} %get-tuple-element.60.refs_5_) | copy-start | bytes 6291460
  15.4 4.6 collective-permute-start.5
  16.2 49.1 %collective-permute-start.6 = (bf16[1,512,2048]{2,1,0:T(8,128)(2,1)}, bf16[1,512,2048]{2,1,0:T(8,128)(2,1)}, u32[]{:S(2)}, u32[]{:S(2)}) collective-permute-start(bf16[1,512,2048]{2,1,0:T(8,128)(2,1)} %get-tuple-element.65.refs_0_), channel_id=1, source_target_pairs={{0,2},{1,3},{2,0},{3,1},{4,6},{5,7},{6,4},{7,5}} | collective-permute-start | bytes 6291464 | tf_op jit(solution)/shard_map/ppermute | solution.py:187
  18.7 137.9 %collective-permute-start = (bf16[1,512,2048]{2,1,0:T(8,128)(2,1)}, bf16[1,512,2048]{2,1,0:T(8,128)(2,1)}, u32[]{:S(2)}, u32[]{:S(2)}) collective-permute-start(bf16[1,512,2048]{2,1,0:T(8,128)(2,1)} %get-tuple-element.65.refs_0_), channel_id=1, source_target_pairs={{0,1},{1,0},{2,3},{3,2},{4,5},{5,4},{6,7},{7,6}} | collective-permute-start | bytes 6291464 | tf_op jit(solution)/shard_map/ppermute | solution.py:187
  18.9 133.6 %collective-permute-start.1 = (bf16[1,512,2048]{2,1,0:T(8,128)(2,1)}, bf16[1,512,2048]{2,1,0:T(8,128)(2,1)}, u32[]{:S(2)}, u32[]{:S(2)}) collective-permute-start(bf16[1,512,2048]{2,1,0:T(8,128)(2,1)} %get-tuple-element.61.refs_1_), channel_id=1, source_target_pairs={{0,1},{1,0},{2,3},{3,2},{4,5},{5,4},{6,7},{7,6}} | collective-permute-start | bytes 6291464 | tf_op jit(solution)/shard_map/ppermute | solution.py:187
  19.2 135.1 %collective-permute-start.2 = (bf16[1,512,2048]{2,1,0:T(8,128)(2,1)}, bf16[1,512,2048]{2,1,0:T(8,128)(2,1)}, u32[]{:S(2)}, u32[]{:S(2)}) collective-permute-start(bf16[1,512,2048]{2,1,0:T(8,128)(2,1)} %get-tuple-element.62.refs_2_), channel_id=1, source_target_pairs={{0,1},{1,0},{2,3},{3,2},{4,5},{5,4},{6,7},{7,6}} | collective-permute-start | bytes 6291464 | tf_op jit(solution)/shard_map/ppermute | solution.py:187
  20.0 1.3 copy-start.3
  21.3 133.3 %collective-permute-start.3 = (bf16[1,512,2048]{2,1,0:T(8,128)(2,1)}, bf16[1,512,2048]{2,1,0:T(8,128)(2,1)}, u32[]{:S(2)}, u32[]{:S(2)}) collective-permute-start(bf16[1,512,2048]{2,1,0:T(8,128)(2,1)} %get-tuple-element.63.refs_3_), channel_id=1, source_target_pairs={{0,1},{1,0},{2,3},{3,2},{4,5},{5,4},{6,7},{7,6}} | collective-permute-start | bytes 6291464 | tf_op jit(solution)/shard_map/ppermute | solution.py:187
  65.3 91.0 %collective-permute-start.4 = (bf16[1,512,2048]{2,1,0:T(8,128)(2,1)}, bf16[1,512,2048]{2,1,0:T(8,128)(2,1)}, u32[]{:S(2)}, u32[]{:S(2)}) collective-permute-start(bf16[1,512,2048]{2,1,0:T(8,128)(2,1)} %get-tuple-element.64.refs_4_), channel_id=1, source_target_pairs={{0,1},{1,0},{2,3},{3,2},{4,5},{5,4},{6,7},{7,6}} | collective-permute-start | bytes 6291464 | tf_op jit(solution)/shard_map/ppermute | solution.py:187
  152.6 305.7 %collective-permute-start.15 = (bf16[1,512,2048]{2,1,0:T(8,128)(2,1)}, bf16[1,512,2048]{2,1,0:T(8,128)(2,1)}, u32[]{:S(2)}, u32[]{:S(2)}) collective-permute-start(bf16[1,512,2048]{2,1,0:T(8,128)(2,1)} %copy-done.2), channel_id=1, source_target_pairs={{0,2},{1,3},{2,0},{3,1},{4,6},{5,7},{6,4},{7,5}} | collective-permute-start | bytes 6291464 | tf_op jit(solution)/shard_map/ppermute | solution.py:187
  154.3 103.9 %collective-permute-start.7 = (bf16[1,512,2048]{2,1,0:T(8,128)(2,1)}, bf16[1,512,2048]{2,1,0:T(8,128)(2,1)}, u32[]{:S(2)}, u32[]{:S(2)}) collective-permute-start(bf16[1,512,2048]{2,1,0:T(8,128)(2,1)} %get-tuple-element.61.refs_1_), channel_id=1, source_target_pairs={{0,2},{1,3},{2,0},{3,1},{4,6},{5,7},{6,4},{7,5}} | collective-permute-start | bytes 6291464 | tf_op jit(solution)/shard_map/ppermute | solution.py:187
  154.6 136.7 %collective-permute-start.8 = (bf16[1,512,2048]{2,1,0:T(8,128)(2,1)}, bf16[1,512,2048]{2,1,0:T(8,128)(2,1)}, u32[]{:S(2)}, u32[]{:S(2)}) collective-permute-start(bf16[1,512,2048]{2,1,0:T(8,128)(2,1)} %get-tuple-element.62.refs_2_), channel_id=1, source_target_pairs={{0,2},{1,3},{2,0},{3,1},{4,6},{5,7},{6,4},{7,5}} | collective-permute-start | bytes 6291464 | tf_op jit(solution)/shard_map/ppermute | solution.py:187
  156.3 179.9 %collective-permute-start.9 = (bf16[1,512,2048]{2,1,0:T(8,128)(2,1)}, bf16[1,512,2048]{2,1,0:T(8,128)(2,1)}, u32[]{:S(2)}, u32[]{:S(2)}) collective-permute-start(bf16[1,512,2048]{2,1,0:T(8,128)(2,1)} %get-tuple-element.63.refs_3_), channel_id=1, source_target_pairs={{0,2},{1,3},{2,0},{3,1},{4,6},{5,7},{6,4},{7,5}} | collective-permute-start | bytes 6291464 | tf_op jit(solution)/shard_map/ppermute | solution.py:187
  156.6 180.1 %collective-permute-start.13 = (bf16[1,512,2048]{2,1,0:T(8,128)(2,1)}, bf16[1,512,2048]{2,1,0:T(8,128)(2,1)}, u32[]{:S(2)}, u32[]{:S(2)}) collective-permute-start(bf16[1,512,2048]{2,1,0:T(8,128)(2,1)} %collective-permute-done.6.refs_6_), channel_id=1, source_target_pairs={{0,1},{1,0},{2,3},{3,2},{4,5},{5,4},{6,7},{7,6}} | collective-permute-start | bytes 6291464 | tf_op jit(solution)/shard_map/ppermute | solution.py:187
  258.2 138.4 %collective-permute-start.14 = (bf16[1,512,2048]{2,1,0:T(8,128)(2,1)}, bf16[1,512,2048]{2,1,0:T(8,128)(2,1)S(1)}, u32[]{:S(2)}, u32[]{:S(2)}) collective-permute-start(bf16[1,512,2048]{2,1,0:T(8,128)(2,1)} %get-tuple-element.64.refs_4_), channel_id=1, source_target_pairs={{0,2},{1,3},{2,0},{3,1},{4,6},{5,7},{6,4},{7,5}} | collective-permute-start | bytes 6291464 | tf_op jit(solution)/shard_map/ppermute | solution.py:187
  336.2 62.3 %collective-permute-start.10 = (bf16[1,512,2048]{2,1,0:T(8,128)(2,1)}, bf16[1,512,2048]{2,1,0:T(8,128)(2,1)}, u32[]{:S(2)}, u32[]{:S(2)}) collective-permute-start(bf16[1,512,2048]{2,1,0:T(8,128)(2,1)} %collective-permute-done.7.refs_1_), channel_id=1, source_target_pairs={{0,1},{1,0},{2,3},{3,2},{4,5},{5,4},{6,7},{7,6}} | collective-permute-start | bytes 6291464 | tf_op jit(solution)/shard_map/ppermute | solution.py:187
  336.2 62.3 %collective-permute-start.11 = (bf16[1,512,2048]{2,1,0:T(8,128)(2,1)}, bf16[1,512,2048]{2,1,0:T(8,128)(2,1)}, u32[]{:S(2)}, u32[]{:S(2)}) collective-permute-start(bf16[1,512,2048]{2,1,0:T(8,128)(2,1)} %collective-permute-done.8.refs_2_), channel_id=1, source_target_pairs={{0,1},{1,0},{2,3},{3,2},{4,5},{5,4},{6,7},{7,6}} | collective-permute-start | bytes 6291464 | tf_op jit(solution)/shard_map/ppermute | solution.py:187
  336.7 61.8 %collective-permute-start.12 = (bf16[1,512,2048]{2,1,0:T(8,128)(2,1)}, bf16[1,512,2048]{2,1,0:T(8,128)(2,1)}, u32[]{:S(2)}, u32[]{:S(2)}) collective-permute-start(bf16[1,512,2048]{2,1,0:T(8,128)(2,1)} %collective-permute-done.9.refs_3_), channel_id=1, source_target_pairs={{0,1},{1,0},{2,3},{3,2},{4,5},{5,4},{6,7},{7,6}} | collective-permute-start | bytes 6291464 | tf_op jit(solution)/shard_map/ppermute | solution.py:187
  396.7 1.4 copy-start.4
  398.0 60.2 %collective-permute-start.17 = (bf16[1,512,2048]{2,1,0:T(8,128)(2,1)}, bf16[1,512,2048]{2,1,0:T(8,128)(2,1)S(1)}, u32[]{:S(2)}, u32[]{:S(2)}) collective-permute-start(bf16[1,512,2048]{2,1,0:T(8,128)(2,1)} %copy-done.4), channel_id=1, source_target_pairs={{0,1},{1,0},{2,3},{3,2},{4,5},{5,4},{6,7},{7,6}} | collective-permute-start | bytes 6291464 | tf_op jit(solution)/shard_map/ppermute | solution.py:187
  458.2 33.7 %collective-permute-start.16 = (bf16[1,512,2048]{2,1,0:T(8,128)(2,1)}, bf16[1,512,2048]{2,1,0:T(8,128)(2,1)}, u32[]{:S(2)}, u32[]{:S(2)}) collective-permute-start(bf16[1,512,2048]{2,1,0:T(8,128)(2,1)} %collective-permute-done.15.refs_1_), channel_id=1, source_target_pairs={{0,1},{1,0},{2,3},{3,2},{4,5},{5,4},{6,7},{7,6}} | collective-permute-start | bytes 6291464 | tf_op jit(solution)/shard_map/ppermute | solution.py:187
  458.3 1.4 copy-start.1

commit v3 on v2

v3 whole, which is shorter than its diff:
```python
import functools
import jax, jax.numpy as jnp
from jax import lax
from jax.experimental import pallas as pl
from jax.experimental.pallas import tpu as pltpu

from jax.sharding import PartitionSpec as P

NORM_EPS = 1e-6
L, D, HK, TOK = 6, 2048, 512, 512
PIECES, ROWS = 8, 64
SPREAD = 2
NT = D // 256


def proj_body(units, n_src, has_prev, *refs):
    n = len(units)
    srcs = refs[:n_src]
    wk, wv = refs[n_src:n_src + 2]
    ok, ov = refs[n_src + 2 + (2 if has_prev else 0):n_src + 4 + (2 if has_prev else 0)]
    ybuf, wbuf, obuf, y_sem, w_sem, o_sem = refs[-6:]
    me = lax.axis_index("tp")

    def place(layer, u):
        seq, code = unit_scalars(u)
        return layer, seq, jnp.bitwise_xor(me, code) * TOK

    def out_copy(kv, at, slot):
        layer, seq, col = at
        dst = (ok, ov)[kv].at[layer, seq, :, pl.ds(pl.multiple_of(col, TOK), TOK)]
        return pltpu.make_async_copy(obuf.at[kv, slot], dst, o_sem.at[kv])

    def unit_scalars(u):
        seq, code = jnp.int32(units[0][2]), jnp.int32(units[0][3])
        for i in range(1, n):
            seq = jnp.where(u == i, units[i][2], seq)
            code = jnp.where(u == i, units[i][3], code)
        return seq, code

    def w_copy(kv, layer, slot):
        return pltpu.make_async_copy((wk, wv)[kv].at[layer], wbuf.at[slot, kv], w_sem.at[slot, kv])

    def y_copy(u):
        s, i = units[u][:2]
        return pltpu.make_async_copy(srcs[s].at[i], ybuf.at[u], y_sem.at[u])

    def y_wait(u):
        pltpu.make_async_copy(srcs[0].at[0], ybuf.at[u], y_sem.at[u]).wait()

    def run(*accs):
        acc = [[[accs[(kv * 2 + q) * PIECES + p] for p in range(PIECES)] for q in range(2)] for kv in range(2)]

        def push(u, tile, reg):
            for q in range(2):
                pltpu.matmul_push_rhs(ybuf[u, pl.ds(q * 256, 256), pl.ds(tile * 256, 256)], staging_register=reg, mxu_index=q, transpose=True)

        def feed(kv, slot, tile, reg, after):
            for p in range(PIECES):
                lhs = wbuf[slot, kv, pl.ds(p * ROWS, ROWS), pl.ds(tile * 256, 256)]
                for q in range(2):
                    pltpu.matmul_acc_lhs(acc[kv][q][p], lhs, load_staged_rhs=reg if p == 0 else None)
                after(p)

        def drain(kv, p, slot):
            for q in range(2):
                obuf[kv, slot, pl.ds(p * ROWS, ROWS), pl.ds(q * 256, 256)] = pltpu.matmul_pop(acc[kv][q][p]).astype(jnp.bfloat16)

        first = place(0, 0)
        w_copy(0, 0, 0).start()
        y_copy(0).start()
        w_copy(1, 0, 0).start()
        for kv in range(2):
            for p in range(PIECES):
                drain(kv, p, 1)
        out_copy(0, first, 0).start()
        out_copy(1, first, 0).start()
        w_copy(0, 0, 0).wait()
        y_copy(0).wait()
        push(0, 0, 1)
        for p in range(PIECES):
            for q in range(2):
                pltpu.matmul_acc_lhs(acc[1][q][p], jnp.zeros((ROWS, 256), jnp.bfloat16), load_staged_rhs=1 if p == 0 else None)
        push(0, 0, 0)
        for u in range(1, min(n, 2)):
            y_copy(u).start()

        def trip(layer, u, carry, opening):
            last, before = carry
            slot, oslot = layer % 2, (layer * n + u) % 2
            out_copy(0, last, 0).wait()
            out_copy(1, last, 0).wait()
            out_copy(0, last, 1 - oslot).start()
            out_copy(1, before, oslot).start()
            nxt = lax.select(u + 1 == n, 0, u + 1)
            for i in range(2 * NT):
                kv, tile = divmod(i, NT)
                if opening and i == NT:
                    @pl.when(u == 0)
                    def _():
                        w_copy(1, 0, 0).wait()
                        for ahead in range(2):
                            w_copy(ahead, 1, 1).start()

                    for v in range(2, n):
                        @pl.when(u == v - 2)
                        def _():
                            y_copy(v).start()
                if opening and i == 2 * NT - 1:
                    @pl.when(u + 1 < n)
                    def _():
                        y_wait(u + 1)

                def after(p):
                    if p == 0:
                        if i < 2 * NT - 1:
                            push(u, (i + 1) % NT, (i + 1) % 2)
                        else:
                            push(nxt, 0, 0)
                    step = tile * PIECES + p - PIECES
                    if step >= 0 and step % SPREAD == SPREAD - 1 and step // SPREAD < PIECES:
                        drain(1 - kv, step // SPREAD, 1 - oslot if kv == 0 else oslot)

                feed(kv, slot, tile, i % 2, after)
            return place(layer, u), last

        carry = lax.fori_loop(0, n, lambda u, c: trip(0, u, c, True), (first, first))

        def layer_loop(layer, carry):
            slot = layer % 2
            for kv in range(2):
                w_copy(kv, layer, slot).wait()
            nl = jnp.minimum(layer + 1, L - 1)
            for kv in range(2):
                w_copy(kv, nl, 1 - slot).start()
            return lax.fori_loop(0, n, lambda u, c: trip(layer, u, c, False), carry)

        last, before = lax.fori_loop(1, L, layer_loop, carry)
        slot = (L * n - 1) % 2
        for kv in range(2):
            w_copy(kv, L - 1, L % 2).wait()
        out_copy(0, last, 0).wait()
        out_copy(1, last, 0).wait()
        out_copy(0, last, slot).start()
        out_copy(1, before, 1 - slot).start()
        for p in range(PIECES):
            drain(1, p, slot)
        for p in range(PIECES):
            for q in range(2):
                pltpu.matmul_acc_lhs(acc[0][q][p], jnp.zeros((ROWS, 256), jnp.bfloat16), load_staged_rhs=0 if p == 0 else None)
        out_copy(1, last, 0).wait()
        out_copy(1, last, slot).start()
        out_copy(0, last, 0).wait()
        out_copy(1, last, 0).wait()

    pl.run_scoped(run, *[pltpu.ACC(q)((ROWS, 256), jnp.float32) for _ in range(2) for q in range(2) for _ in range(PIECES)])


def project(sources, units, wk, wv, prev):
    n = len(units)
    out = jax.ShapeDtypeStruct((L, 6, HK, 4 * TOK), jnp.bfloat16)
    args = list(sources) + [wk, wv] + (list(prev) if prev else [])
    k = len(sources) + 2
    return pl.pallas_call(
        functools.partial(proj_body, units, len(sources), bool(prev)),
        out_shape=[out, out],
        in_specs=[pl.BlockSpec(memory_space=pl.ANY)] * len(args),
        out_specs=[pl.BlockSpec(memory_space=pl.ANY)] * 2,
        scratch_shapes=[
            pltpu.VMEM((n, TOK, D), jnp.bfloat16),
            pltpu.VMEM((2, 2, HK, D), jnp.bfloat16),
            pltpu.VMEM((2, 2, HK, TOK), jnp.bfloat16),
            pltpu.SemaphoreType.DMA((n,)),
            pltpu.SemaphoreType.DMA((2, 2)),
            pltpu.SemaphoreType.DMA((2,)),
        ],
        input_output_aliases={k: 0, k + 1: 1} if prev else {},
        cost_estimate=pl.CostEstimate(flops=2 * n * TOK * D * HK * 2 * L, bytes_accessed=n * (TOK * D * 2 + 2 * L * HK * TOK * 2) + 4 * L * HK * D, transcendentals=0),
        compiler_params=pltpu.CompilerParams(vmem_limit_bytes=67_000_000, has_side_effects=True),
    )(*args)


CHUNKS = ((0,), (1, 2, 3), (4,), (5,))
NORM_ROWS = 256


def blocks_of(name, *chunks):
    return [(name, c) for c in chunks]


PLAN = [
    (blocks_of("own", 0, 1, 2, 3), (0,)),
    (blocks_of("mate", 0, 1, 2, 3) + blocks_of("far", 0), (1,)),
    (blocks_of("far", 1) + blocks_of("fwd", 0), (2,)),
    (blocks_of("fwd", 1) + blocks_of("far", 2), (3,)),
    (blocks_of("far", 3) + blocks_of("fwd", 2), ()),
    (blocks_of("fwd", 3), ()),
]


def norm_body(x_ref, scale_ref, *outs):
    acts = x_ref[...].astype(jnp.float32)
    mean_sq = jnp.mean(acts * acts, axis=-1, keepdims=True)
    normed = (acts * lax.rsqrt(mean_sq + NORM_EPS) * scale_ref[...].astype(jnp.float32)).astype(jnp.bfloat16)
    block = pl.program_id(0)
    start = 0
    for seqs, out in zip(CHUNKS, outs):
        stop = start + len(seqs) * (TOK // NORM_ROWS)

        @pl.when((block >= start) & (block < stop))
        def _():
            out[...] = normed

        start = stop


def rms_norm(enc_out, norm_scale):
    per_seq = TOK // NORM_ROWS
    specs, start = [], 0
    for seqs in CHUNKS:
        blocks = len(seqs) * per_seq
        specs.append(pl.BlockSpec((1, NORM_ROWS, D), functools.partial(lambda start, blocks, i: (jnp.clip(i - start, 0, blocks - 1) // per_seq, jnp.clip(i - start, 0, blocks - 1) % per_seq, 0), start, blocks)))
        start += blocks
    return pl.pallas_call(
        norm_body,
        grid=(start,),
        out_shape=[jax.ShapeDtypeStruct((len(seqs), TOK, D), jnp.bfloat16) for seqs in CHUNKS],
        in_specs=[pl.BlockSpec((1, NORM_ROWS, D), lambda i: (i // per_seq, i % per_seq, 0)), pl.BlockSpec((1, 1, D), lambda i: (0, 0, 0))],
        out_specs=specs,
        cost_estimate=pl.CostEstimate(flops=start * NORM_ROWS * D * 6, bytes_accessed=start * NORM_ROWS * D * 4, transcendentals=0),
        compiler_params=pltpu.CompilerParams(vmem_limit_bytes=67_000_000),
    )(enc_out, norm_scale.reshape(1, 1, D))


def swap(x, code):
    return lax.ppermute(x, "tp", [(i, i ^ code) for i in range(4)])


def solution(mesh):
    def gather_and_project(enc_out, norm_scale, w_key, w_value):
        wk = jnp.transpose(w_key, (0, 2, 3, 1)).reshape(L, HK, D)
        wv = jnp.transpose(w_value, (0, 2, 3, 1)).reshape(L, HK, D)
        y = rms_norm(enc_out, norm_scale)
        count = len(CHUNKS)
        far = [swap(y[c], 2) for c in range(count)]
        mate = [swap(y[c], 1) for c in range(count)]
        fwd = [None] * count
        kept = {"own": y, "mate": mate, "far": far, "fwd": fwd}
        code = {"own": 0, "mate": 1, "far": 2, "fwd": 3}
        out = None
        for group, forward in PLAN:
            sources = [kept[name][c] for name, c in group]
            units = [(s, i, seq, code[name]) for s, (name, c) in enumerate(group) for i, seq in enumerate(CHUNKS[c])]
            out = project(sources, units, wk, wv, out)
            if forward:
                out, moved = lax.optimization_barrier((out, [far[c] for c in forward]))
                for c, block in zip(forward, moved):
                    far[c] = block
                    fwd[c] = swap(block, 1)
        return tuple(jnp.transpose(o.reshape(L, 6, 8, 64, 4 * TOK), (0, 1, 4, 2, 3)) for o in out)

    weight_spec = P(None, None, "tp", None)
    cache_spec = P(None, "dp", None, "tp", None)
    return jax.shard_map(gather_and_project, mesh=mesh, in_specs=(P("dp", "tp", None), P(None), weight_spec, weight_spec), out_specs=(cache_spec, cache_spec), check_vma=False)
```

time: 513 us -> 414 us (0.81)
  waiting for transfers between devices: 120 us -> 40.3 us
  other arithmetic: 12.6 us -> 0 us
    ppermute x18 -> x12, waiting for transfers between devices: 120 us -> 40.3 us  [swap(): return lax.ppermute(x, 'tp', [(i, i ^ code) for i in range(4)])]
    pallas_call x0 -> x1, Pallas kernels: none -> 15.3 us  [rms_norm(): pl.pallas_call(norm_body, grid=(start,), out_shape=[jax.ShapeDtypeStruct(...]
    pallas_call x6, Pallas kernels: 361 us -> 349 us  [project(): pl.pallas_call(functools.partial(proj_body, units, len(sources), bool(pre...]
    convert_element_type x2 -> x0, other arithmetic: 6.51 us -> none  [the longest x1 5.82 us: rms_norm(): (acts * lax.rsqrt(mean_sq + NORM_EPS) * norm_scale.astype(jnp.float32)).a...]
    unnamed x10 -> x0, local copies, waits for them, and re-layouts: 6.16 us -> none
    reduce_sum x1 -> x0, other arithmetic: 6.04 us -> none  [rms_norm(): mean_sq = jnp.mean(acts * acts, axis=-1, keepdims=True)]
    ppermute x18 -> x12, starting transfers between devices: 11.3 us -> 6.95 us  [swap(): return lax.ppermute(x, 'tp', [(i, i ^ code) for i in range(4)])]
  transfers between devices with their start and end apart: 18 -> 12, of which waited for: 4 -> 1; matrix products, arithmetic and copies ran while one was open for 0% -> 0% of each run, Pallas kernels for 66% -> 79%
where the time goes in v3:
time: 414 us
  Pallas kernels  365 us (88%)
  waiting for transfers between devices  40.3 us (10%)
  starting transfers between devices  6.95 us (2%)
    pallas_call x6, Pallas kernels, project(): pl.pallas_call(functools.partial(proj_body, units, len(sources), bool(pre...  349 us
    ppermute x12, waiting for transfers between devices, swap(): return lax.ppermute(x, 'tp', [(i, i ^ code) for i in range(4)])  40.3 us
    pallas_call x1, Pallas kernels, rms_norm(): pl.pallas_call(norm_body, grid=(start,), out_shape=[jax.ShapeDtypeStruct(...  15.3 us
  transfers between devices with their start and end apart: 12, of which 1 were waited for; matrix products, arithmetic and copies ran while one was open for 0% of the time, Pallas kernels for 79%

profile of v3, /device:TPU:0, one launch (start us, length us, event | category | flops | bytes accessed | tf_op | source)
XLA Modules:
  0.0 414.0 jit_solution(9770903079003507485)
XLA Ops:
  0.6 1.3 reshape.19.scale_ref
  1.9 15.3 %shard_map.59 = (bf16[1,512,2048]{2,1,0:T(8,128)(2,1)}, bf16[3,512,2048]{2,1,0:T(8,128)(2,1)}, bf16[1,512,2048]{2,1,0:T(8,128)(2,1)}, bf16[1,512,2048]{2,1,0:T(8,128)(2,1)}) custom-call(bf16[6,512,2048]{2,1,0:T(8,128)(2,1)} %x_ref.1, bf16[1,1,2048]{2,1,0:T(2,128)(2,1)} %reshape.19.scale_ref), custom_call_target="tpu_custom_call" | custom-call | flops 37748736 | bytes 25165824 | tf_op jit(solution)/shard_map/pallas_call | solution.py:223
  17.3 3.3 collective-permute-start.4
  20.6 0.0 collective-permute-start
  20.6 0.5 collective-permute-start.2
  21.1 0.0 collective-permute-start.3
  21.1 0.5 collective-permute-start.1
  21.6 84.1 %shard_map.60 = (bf16[6,6,512,2048]{3,2,1,0:T(8,128)(2,1)}, bf16[6,6,512,2048]{3,2,1,0:T(8,128)(2,1)}) custom-call(bf16[1,512,2048]{2,1,0:T(8,128)(2,1)} %get-tuple-element.30.refs_0_, bf16[3,512,2048]{2,1,0:T(8,128)(2,1)} %get-tuple-element.31.refs_1_, bf16[1,512,2048]{2,1,0:T(8,128)(2,1)} %get-tuple-element.32.refs_2_, ...), custom_call_target="tpu_custom_call" | custom-call | flops 77309411328 | bytes 75497472 | tf_op jit(solution)/shard_map/pallas_call | solution.py:163
  105.8 0.0 collective-permute-start.5
  105.8 0.0 collective-permute-done.refs_0_
  105.8 0.0 collective-permute-start.7
  105.8 0.0 collective-permute-done.2.refs_2_
  105.9 97.4 %shard_map.61 = (bf16[6,6,512,2048]{3,2,1,0:T(8,128)(2,1)}, bf16[6,6,512,2048]{3,2,1,0:T(8,128)(2,1)}) custom-call(bf16[1,512,2048]{2,1,0:T(8,128)(2,1)} %collective-permute-done.refs_0_, bf16[3,512,2048]{2,1,0:T(8,128)(2,1)} %collective-permute-done.1.refs_1_, ...), custom_call_target="tpu_custom_call", output_to_operand_aliasing={{0}: (7, {}), {1}: (8, {})} | custom-call | flops 90194313216 | bytes 83886080 | tf_op jit(solution)/shard_map/pallas_call | solution.py:163
  203.3 40.2 %collective-permute-done.5.refs_0_ = bf16[3,512,2048]{2,1,0:T(8,128)(2,1)} collective-permute-done((bf16[3,512,2048]{2,1,0:T(8,128)(2,1)}, bf16[3,512,2048]{2,1,0:T(8,128)(2,1)}, u32[]{:S(2)}, u32[]{:S(2)}) %collective-permute-start.5) | collective-permute-done | bytes 6291488 | tf_op jit(solution)/shard_map/ppermute | solution.py:235
  243.5 0.0 collective-permute-start.6
  243.5 0.3 collective-permute-start.8
  243.8 1.7 collective-permute-start.9
  245.6 57.7 %shard_map.62 = (bf16[6,6,512,2048]{3,2,1,0:T(8,128)(2,1)}, bf16[6,6,512,2048]{3,2,1,0:T(8,128)(2,1)}) custom-call(bf16[3,512,2048]{2,1,0:T(8,128)(2,1)} %collective-permute-done.5.refs_0_, bf16[1,512,2048]{2,1,0:T(8,128)(2,1)} %collective-permute-done.7.refs_1_, bf16[6,512,2048]{2,1,0:T(8,128)(2,1)} %bitcast.14, ...), custom_call_target="tpu_custom_call", output_to_operand_aliasing={{0}: (4, {}), {1}: (5, {})} | custom-call | flops 51539607552 | bytes 58720256 | tf_op jit(solution)/shard_map/pallas_call | solution.py:163
  303.2 0.0 collective-permute-start.11
  303.3 57.9 %shard_map.63 = (bf16[6,6,512,2048]{3,2,1,0:T(8,128)(2,1)}, bf16[6,6,512,2048]{3,2,1,0:T(8,128)(2,1)}) custom-call(bf16[3,512,2048]{2,1,0:T(8,128)(2,1)} %collective-permute-done.6.refs_0_, bf16[1,512,2048]{2,1,0:T(8,128)(2,1)} %collective-permute-done.8.refs_1_, bf16[6,512,2048]{2,1,0:T(8,128)(2,1)} %bitcast.15, ...), custom_call_target="tpu_custom_call", output_to_operand_aliasing={{0}: (4, {}), {1}: (5, {})} | custom-call | flops 51539607552 | bytes 58720256 | tf_op jit(solution)/shard_map/pallas_call | solution.py:163
  361.2 0.0 collective-permute-done.9.refs_0_
  361.2 0.5 collective-permute-start.10
  361.7 31.2 %shard_map.64 = (bf16[6,6,512,2048]{3,2,1,0:T(8,128)(2,1)}, bf16[6,6,512,2048]{3,2,1,0:T(8,128)(2,1)}) custom-call(bf16[1,512,2048]{2,1,0:T(8,128)(2,1)} %collective-permute-done.9.refs_0_, bf16[1,512,2048]{2,1,0:T(8,128)(2,1)} %collective-permute-done.11.refs_1_, bf16[6,512,2048]{2,1,0:T(8,128)(2,1)} %bitcast.16, ...), custom_call_target="tpu_custom_call", output_to_operand_aliasing={{0}: (4, {}), {1}: (5, {})} | custom-call | flops 25769803776 | bytes 41943040 | tf_op jit(solution)/shard_map/pallas_call | solution.py:163
  392.9 20.9 %shard_map.65 = (bf16[6,6,512,2048]{3,2,1,0:T(8,128)(2,1)}, bf16[6,6,512,2048]{3,2,1,0:T(8,128)(2,1)}) custom-call(bf16[1,512,2048]{2,1,0:T(8,128)(2,1)} %collective-permute-done.10.refs_0_, bf16[6,512,2048]{2,1,0:T(8,128)(2,1)} %bitcast.17, bf16[6,512,2048]{2,1,0:T(8,128)(2,1)} %bitcast.23, ...), custom_call_target="tpu_custom_call", output_to_operand_aliasing={{0}: (3, {}), {1}: (4, {})} | custom-call | flops 12884901888 | bytes 33554432 | tf_op jit(solution)/shard_map/pallas_call | solution.py:163
  (8 shorter events, 0.0 us)
Async XLA Ops:
  17.3 88.5 %collective-permute-start.4 = (bf16[1,512,2048]{2,1,0:T(8,128)(2,1)}, bf16[1,512,2048]{2,1,0:T(8,128)(2,1)}, u32[]{:S(2)}, u32[]{:S(2)}) collective-permute-start(bf16[1,512,2048]{2,1,0:T(8,128)(2,1)} %get-tuple-element.30.refs_0_), channel_id=1, source_target_pairs={{0,2},{1,3},{2,0},{3,1},{4,6},{5,7},{6,4},{7,5}} | collective-permute-start | bytes 6291464 | tf_op jit(solution)/shard_map/ppermute | solution.py:235
  20.6 85.2 %collective-permute-start = (bf16[1,512,2048]{2,1,0:T(8,128)(2,1)}, bf16[1,512,2048]{2,1,0:T(8,128)(2,1)}, u32[]{:S(2)}, u32[]{:S(2)}) collective-permute-start(bf16[1,512,2048]{2,1,0:T(8,128)(2,1)} %get-tuple-element.30.refs_0_), channel_id=1, source_target_pairs={{0,1},{1,0},{2,3},{3,2},{4,5},{5,4},{6,7},{7,6}} | collective-permute-start | bytes 6291464 | tf_op jit(solution)/shard_map/ppermute | solution.py:235
  20.6 85.3 %collective-permute-start.2 = (bf16[1,512,2048]{2,1,0:T(8,128)(2,1)}, bf16[1,512,2048]{2,1,0:T(8,128)(2,1)}, u32[]{:S(2)}, u32[]{:S(2)}) collective-permute-start(bf16[1,512,2048]{2,1,0:T(8,128)(2,1)} %get-tuple-element.32.refs_2_), channel_id=1, source_target_pairs={{0,1},{1,0},{2,3},{3,2},{4,5},{5,4},{6,7},{7,6}} | collective-permute-start | bytes 6291464 | tf_op jit(solution)/shard_map/ppermute | solution.py:235
  21.1 84.8 %collective-permute-start.3 = (bf16[1,512,2048]{2,1,0:T(8,128)(2,1)}, bf16[1,512,2048]{2,1,0:T(8,128)(2,1)}, u32[]{:S(2)}, u32[]{:S(2)}) collective-permute-start(bf16[1,512,2048]{2,1,0:T(8,128)(2,1)} %get-tuple-element.33.refs_3_), channel_id=1, source_target_pairs={{0,1},{1,0},{2,3},{3,2},{4,5},{5,4},{6,7},{7,6}} | collective-permute-start | bytes 6291464 | tf_op jit(solution)/shard_map/ppermute | solution.py:235
  21.1 84.8 %collective-permute-start.1 = (bf16[3,512,2048]{2,1,0:T(8,128)(2,1)}, bf16[3,512,2048]{2,1,0:T(8,128)(2,1)}, u32[]{:S(2)}, u32[]{:S(2)}) collective-permute-start(bf16[3,512,2048]{2,1,0:T(8,128)(2,1)} %get-tuple-element.31.refs_1_), channel_id=1, source_target_pairs={{0,1},{1,0},{2,3},{3,2},{4,5},{5,4},{6,7},{7,6}} | collective-permute-start | bytes 18874376 | tf_op jit(solution)/shard_map/ppermute | solution.py:235
  105.8 137.8 %collective-permute-start.5 = (bf16[3,512,2048]{2,1,0:T(8,128)(2,1)}, bf16[3,512,2048]{2,1,0:T(8,128)(2,1)}, u32[]{:S(2)}, u32[]{:S(2)}) collective-permute-start(bf16[3,512,2048]{2,1,0:T(8,128)(2,1)} %get-tuple-element.31.refs_1_), channel_id=1, source_target_pairs={{0,2},{1,3},{2,0},{3,1},{4,6},{5,7},{6,4},{7,5}} | collective-permute-start | bytes 18874376 | tf_op jit(solution)/shard_map/ppermute | solution.py:235
  105.8 139.7 %collective-permute-start.7 = (bf16[1,512,2048]{2,1,0:T(8,128)(2,1)}, bf16[1,512,2048]{2,1,0:T(8,128)(2,1)}, u32[]{:S(2)}, u32[]{:S(2)}) collective-permute-start(bf16[1,512,2048]{2,1,0:T(8,128)(2,1)} %collective-permute-done.4.refs_4_), channel_id=1, source_target_pairs={{0,1},{1,0},{2,3},{3,2},{4,5},{5,4},{6,7},{7,6}} | collective-permute-start | bytes 6291464 | tf_op jit(solution)/shard_map/ppermute | solution.py:235
  243.5 59.8 %collective-permute-start.6 = (bf16[3,512,2048]{2,1,0:T(8,128)(2,1)}, bf16[3,512,2048]{2,1,0:T(8,128)(2,1)}, u32[]{:S(2)}, u32[]{:S(2)}) collective-permute-start(bf16[3,512,2048]{2,1,0:T(8,128)(2,1)} %collective-permute-done.5.refs_0_), channel_id=1, source_target_pairs={{0,1},{1,0},{2,3},{3,2},{4,5},{5,4},{6,7},{7,6}} | collective-permute-start | bytes 18874376 | tf_op jit(solution)/shard_map/ppermute | solution.py:235
  243.5 59.7 %collective-permute-start.8 = (bf16[1,512,2048]{2,1,0:T(8,128)(2,1)}, bf16[1,512,2048]{2,1,0:T(8,128)(2,1)}, u32[]{:S(2)}, u32[]{:S(2)}) collective-permute-start(bf16[1,512,2048]{2,1,0:T(8,128)(2,1)} %get-tuple-element.32.refs_2_), channel_id=1, source_target_pairs={{0,2},{1,3},{2,0},{3,1},{4,6},{5,7},{6,4},{7,5}} | collective-permute-start | bytes 6291464 | tf_op jit(solution)/shard_map/ppermute | solution.py:235
  243.8 117.4 %collective-permute-start.9 = (bf16[1,512,2048]{2,1,0:T(8,128)(2,1)}, bf16[1,512,2048]{2,1,0:T(8,128)(2,1)}, u32[]{:S(2)}, u32[]{:S(2)}) collective-permute-start(bf16[1,512,2048]{2,1,0:T(8,128)(2,1)} %get-tuple-element.33.refs_3_), channel_id=1, source_target_pairs={{0,2},{1,3},{2,0},{3,1},{4,6},{5,7},{6,4},{7,5}} | collective-permute-start | bytes 6291464 | tf_op jit(solution)/shard_map/ppermute | solution.py:235
  303.2 58.4 %collective-permute-start.11 = (bf16[1,512,2048]{2,1,0:T(8,128)(2,1)}, bf16[1,512,2048]{2,1,0:T(8,128)(2,1)}, u32[]{:S(2)}, u32[]{:S(2)}) collective-permute-start(bf16[1,512,2048]{2,1,0:T(8,128)(2,1)} %collective-permute-done.8.refs_1_), channel_id=1, source_target_pairs={{0,1},{1,0},{2,3},{3,2},{4,5},{5,4},{6,7},{7,6}} | collective-permute-start | bytes 6291464 | tf_op jit(solution)/shard_map/ppermute | solution.py:235
  361.2 31.7 %collective-permute-start.10 = (bf16[1,512,2048]{2,1,0:T(8,128)(2,1)}, bf16[1,512,2048]{2,1,0:T(8,128)(2,1)}, u32[]{:S(2)}, u32[]{:S(2)}) collective-permute-start(bf16[1,512,2048]{2,1,0:T(8,128)(2,1)} %collective-permute-done.9.refs_0_), channel_id=1, source_target_pairs={{0,1},{1,0},{2,3},{3,2},{4,5},{5,4},{6,7},{7,6}} | collective-permute-start | bytes 6291464 | tf_op jit(solution)/shard_map/ppermute | solution.py:235

commit v4 on v3

--- a/solution.py
+++ b/solution.py
@@ -180,7 +180,6 @@
 
 
 CHUNKS = ((0,), (1, 2, 3), (4,), (5,))
-NORM_ROWS = 256
 
 
 def blocks_of(name, *chunks):
@@ -191,44 +190,16 @@
     (blocks_of("own", 0, 1, 2, 3), (0,)),
     (blocks_of("mate", 0, 1, 2, 3) + blocks_of("far", 0), (1,)),
     (blocks_of("far", 1) + blocks_of("fwd", 0), (2,)),
-    (blocks_of("fwd", 1) + blocks_of("far", 2), (3,)),
-    (blocks_of("far", 3) + blocks_of("fwd", 2), ()),
-    (blocks_of("fwd", 3), ()),
+    (blocks_of("fwd", 1), (3,)),
+    (blocks_of("far", 2) + blocks_of("fwd", 2), ()),
+    (blocks_of("far", 3) + blocks_of("fwd", 3), ()),
 ]
 
 
-def norm_body(x_ref, scale_ref, *outs):
-    acts = x_ref[...].astype(jnp.float32)
+def rms_norm(enc_out, norm_scale):
+    acts = enc_out.astype(jnp.float32)
     mean_sq = jnp.mean(acts * acts, axis=-1, keepdims=True)
-    normed = (acts * lax.rsqrt(mean_sq + NORM_EPS) * scale_ref[...].astype(jnp.float32)).astype(jnp.bfloat16)
-    block = pl.program_id(0)
-    start = 0
-    for seqs, out in zip(CHUNKS, outs):
-        stop = start + len(seqs) * (TOK // NORM_ROWS)
-
-        @pl.when((block >= start) & (block < stop))
-        def _():
-            out[...] = normed
-
-        start = stop
-
-
-def rms_norm(enc_out, norm_scale):
-    per_seq = TOK // NORM_ROWS
-    specs, start = [], 0
-    for seqs in CHUNKS:
-        blocks = len(seqs) * per_seq
-        specs.append(pl.BlockSpec((1, NORM_ROWS, D), functools.partial(lambda start, blocks, i: (jnp.clip(i - start, 0, blocks - 1) // per_seq, jnp.clip(i - start, 0, blocks - 1) % per_seq, 0), start, blocks)))
-        start += blocks
-    return pl.pallas_call(
-        norm_body,
-        grid=(start,),
-        out_shape=[jax.ShapeDtypeStruct((len(seqs), TOK, D), jnp.bfloat16) for seqs in CHUNKS],
-        in_specs=[pl.BlockSpec((1, NORM_ROWS, D), lambda i: (i // per_seq, i % per_seq, 0)), pl.BlockSpec((1, 1, D), lambda i: (0, 0, 0))],
-        out_specs=specs,
-        cost_estimate=pl.CostEstimate(flops=start * NORM_ROWS * D * 6, bytes_accessed=start * NORM_ROWS * D * 4, transcendentals=0),
-        compiler_params=pltpu.CompilerParams(vmem_limit_bytes=67_000_000),
-    )(enc_out, norm_scale.reshape(1, 1, D))
+    return (acts * lax.rsqrt(mean_sq + NORM_EPS) * norm_scale.astype(jnp.float32)).astype(jnp.bfloat16)
 
 
 def swap(x, code):
@@ -239,7 +210,7 @@
     def gather_and_project(enc_out, norm_scale, w_key, w_value):
         wk = jnp.transpose(w_key, (0, 2, 3, 1)).reshape(L, HK, D)
         wv = jnp.transpose(w_value, (0, 2, 3, 1)).reshape(L, HK, D)
-        y = rms_norm(enc_out, norm_scale)
+        y = [rms_norm(enc_out[seqs[0] : seqs[-1] + 1], norm_scale) for seqs in CHUNKS]
         count = len(CHUNKS)
         far = [swap(y[c], 2) for c in range(count)]
         mate = [swap(y[c], 1) for c in range(count)]

time: 414 us -> 443 us (1.070)
  waiting for transfers between devices: 40.3 us -> 72.3 us
  Pallas kernels: 365 us -> 347 us
  other arithmetic: 0 us -> 14.8 us
    ppermute x12, waiting for transfers between devices: 40.3 us -> 72.3 us  [swap(): return lax.ppermute(x, 'tp', [(i, i ^ code) for i in range(4)])]
    pallas_call x1 -> x0, Pallas kernels: 15.3 us -> none  [rms_norm(): pl.pallas_call(norm_body, grid=(start,), out_shape=[jax.ShapeDtypeStruct(...]
    convert_element_type x0 -> x3, other arithmetic: none -> 10 us  [the longest x2 9.99 us: rms_norm(): (acts * lax.rsqrt(mean_sq + NORM_EPS) * norm_scale.astype(jnp.float32)).a...]
    reduce_sum x0 -> x2, other arithmetic: none -> 4.8 us  [rms_norm(): mean_sq = jnp.mean(acts * acts, axis=-1, keepdims=True)]
  transfers between devices with their start and end apart: 12 -> 12, of which waited for: 1 -> 2; matrix products, arithmetic and copies ran while one was open for 0% -> 1% of each run, Pallas kernels for 79% -> 71%
where the time goes in v4:
time: 443 us
  Pallas kernels  347 us (78%)
  waiting for transfers between devices  72.3 us (16%)
  other arithmetic  14.8 us (3%)
  starting transfers between devices  8.55 us (2%)
    pallas_call x6, Pallas kernels, project(): pl.pallas_call(functools.partial(proj_body, units, len(sources), bool(pre...  347 us
    ppermute x12, waiting for transfers between devices, swap(): return lax.ppermute(x, 'tp', [(i, i ^ code) for i in range(4)])  72.3 us
    convert_element_type x2, other arithmetic, rms_norm(): (acts * lax.rsqrt(mean_sq + NORM_EPS) * norm_scale.astype(jnp.float32)).a...  9.99 us
  transfers between devices with their start and end apart: 12, of which 2 were waited for; matrix products, arithmetic and copies ran while one was open for 1% of the time, Pallas kernels for 71%

profile of v4, /device:TPU:0, one launch (start us, length us, event | category | flops | bytes accessed | tf_op | source)
XLA Modules:
  0.0 443.1 jit_solution(8463036021660941322)
XLA Ops:
  0.6 3.5 fusion.9
  4.2 0.0 copy-start
  4.2 6.2 %fusion.11 = (bf16[1,512,2048]{2,1,0:T(8,128)(2,1)}, bf16[1,512,2048]{2,1,0:T(8,128)(2,1)}, bf16[1,512,2048]{2,1,0:T(8,128)(2,1)}) fusion(f32[512]{0:T(512)S(1)} %get-tuple-element.56, f32[2048]{0:T(1024)S(1)} %convert_element_type.31, bf16[6,512,2048]{2,1,0:T(8,128)(2,1)} %param.4, f32[512]{0:T(512)S(1)} %get-tuple-element.57, f32[512]{0:T(512)S(1)} %add_rsqrt_fusion.3), kind=kLoop, calls=%fused_computation.19 | loop fusion | flops 12582912 | bytes 12597248 | tf_op jit(solution)/shard_map/convert_element_type | solution.py:202
  10.4 3.3 collective-permute-start.4
  13.7 0.0 collective-permute-start
  13.7 0.5 collective-permute-start.3
  14.2 1.3 fusion
  15.6 3.8 fusion.2.refs_1_
  19.3 0.5 collective-permute-start.1
  19.8 84.1 %shard_map.59 = (bf16[6,6,512,2048]{3,2,1,0:T(8,128)(2,1)}, bf16[6,6,512,2048]{3,2,1,0:T(8,128)(2,1)}) custom-call(bf16[1,512,2048]{2,1,0:T(8,128)(2,1)} %get-tuple-element.55.refs_0_, bf16[3,512,2048]{2,1,0:T(8,128)(2,1)} %fusion.2.refs_1_, bf16[1,512,2048]{2,1,0:T(8,128)(2,1)} %get-tuple-element.54.refs_2_, ...), custom_call_target="tpu_custom_call" | custom-call | flops 77309411328 | bytes 75497472 | tf_op jit(solution)/shard_map/pallas_call | solution.py:163
  104.0 0.0 collective-permute-done.4.refs_4_
  104.0 1.4 collective-permute-start.5
  105.4 0.0 collective-permute-done.3.refs_3_
  105.4 0.2 collective-permute-start.7
  105.7 97.4 %shard_map.60 = (bf16[6,6,512,2048]{3,2,1,0:T(8,128)(2,1)}, bf16[6,6,512,2048]{3,2,1,0:T(8,128)(2,1)}) custom-call(bf16[1,512,2048]{2,1,0:T(8,128)(2,1)} %collective-permute-done.refs_0_, bf16[3,512,2048]{2,1,0:T(8,128)(2,1)} %collective-permute-done.1.refs_1_, ...), custom_call_target="tpu_custom_call", output_to_operand_aliasing={{0}: (7, {}), {1}: (8, {})} | custom-call | flops 90194313216 | bytes 83886080 | tf_op jit(solution)/shard_map/pallas_call | solution.py:163
  203.1 38.9 %collective-permute-done.5.refs_0_ = bf16[3,512,2048]{2,1,0:T(8,128)(2,1)} collective-permute-done((bf16[3,512,2048]{2,1,0:T(8,128)(2,1)}, bf16[3,512,2048]{2,1,0:T(8,128)(2,1)}, u32[]{:S(2)}, u32[]{:S(2)}) %collective-permute-start.5) | collective-permute-done | bytes 6291488 | tf_op jit(solution)/shard_map/ppermute | solution.py:206
  241.9 1.7 collective-permute-start.9
  243.7 0.3 collective-permute-start.8
  244.0 57.9 %shard_map.61 = (bf16[6,6,512,2048]{3,2,1,0:T(8,128)(2,1)}, bf16[6,6,512,2048]{3,2,1,0:T(8,128)(2,1)}) custom-call(bf16[3,512,2048]{2,1,0:T(8,128)(2,1)} %collective-permute-done.5.refs_0_, bf16[1,512,2048]{2,1,0:T(8,128)(2,1)} %collective-permute-done.7.refs_1_, bf16[6,512,2048]{2,1,0:T(8,128)(2,1)} %bitcast.14, ...), custom_call_target="tpu_custom_call", output_to_operand_aliasing={{0}: (4, {}), {1}: (5, {})} | custom-call | flops 51539607552 | bytes 58720256 | tf_op jit(solution)/shard_map/pallas_call | solution.py:163
  301.9 33.4 %collective-permute-done.8.refs_0_ = bf16[1,512,2048]{2,1,0:T(8,128)(2,1)} collective-permute-done((bf16[1,512,2048]{2,1,0:T(8,128)(2,1)}, bf16[1,512,2048]{2,1,0:T(8,128)(2,1)}, u32[]{:S(2)}, u32[]{:S(2)}) %collective-permute-start.8) | collective-permute-done | bytes 2097184 | tf_op jit(solution)/shard_map/ppermute | solution.py:206
  335.2 44.7 %shard_map.62 = (bf16[6,6,512,2048]{3,2,1,0:T(8,128)(2,1)}, bf16[6,6,512,2048]{3,2,1,0:T(8,128)(2,1)}) custom-call(bf16[3,512,2048]{2,1,0:T(8,128)(2,1)} %collective-permute-done.6.refs_0_, bf16[6,512,2048]{2,1,0:T(8,128)(2,1)} %bitcast.15, bf16[6,512,2048]{2,1,0:T(8,128)(2,1)} %bitcast.21, ...), custom_call_target="tpu_custom_call", output_to_operand_aliasing={{0}: (3, {}), {1}: (4, {})} | custom-call | flops 38654705664 | bytes 50331648 | tf_op jit(solution)/shard_map/pallas_call | solution.py:163
  380.0 0.5 collective-permute-start.10
  380.5 31.2 %shard_map.63 = (bf16[6,6,512,2048]{3,2,1,0:T(8,128)(2,1)}, bf16[6,6,512,2048]{3,2,1,0:T(8,128)(2,1)}) custom-call(bf16[1,512,2048]{2,1,0:T(8,128)(2,1)} %collective-permute-done.8.refs_0_, bf16[1,512,2048]{2,1,0:T(8,128)(2,1)} %collective-permute-done.11.refs_1_, bf16[6,512,2048]{2,1,0:T(8,128)(2,1)} %bitcast.16, ...), custom_call_target="tpu_custom_call", output_to_operand_aliasing={{0}: (4, {}), {1}: (5, {})} | custom-call | flops 25769803776 | bytes 41943040 | tf_op jit(solution)/shard_map/pallas_call | solution.py:163
  411.7 31.2 %shard_map.64 = (bf16[6,6,512,2048]{3,2,1,0:T(8,128)(2,1)}, bf16[6,6,512,2048]{3,2,1,0:T(8,128)(2,1)}) custom-call(bf16[1,512,2048]{2,1,0:T(8,128)(2,1)} %collective-permute-done.9.refs_0_, bf16[1,512,2048]{2,1,0:T(8,128)(2,1)} %collective-permute-done.10.refs_1_, bf16[6,512,2048]{2,1,0:T(8,128)(2,1)} %bitcast.17, ...), custom_call_target="tpu_custom_call", output_to_operand_aliasing={{0}: (4, {}), {1}: (5, {})} | custom-call | flops 25769803776 | bytes 41943040 | tf_op jit(solution)/shard_map/pallas_call | solution.py:163
  (18 shorter events, 0.1 us)
Async XLA Ops:
  0.6 3.5 copy-start.1
  4.2 10.1 %copy-start = (bf16[6,512,2048]{2,1,0:T(8,128)(2,1)S(1)}, bf16[6,512,2048]{2,1,0:T(8,128)(2,1)}, u32[]{:S(2)}) copy-start(bf16[6,512,2048]{2,1,0:T(8,128)(2,1)} %param.4) | copy-start | bytes 37748740
  10.4 93.6 %collective-permute-start.4 = (bf16[1,512,2048]{2,1,0:T(8,128)(2,1)}, bf16[1,512,2048]{2,1,0:T(8,128)(2,1)}, u32[]{:S(2)}, u32[]{:S(2)}) collective-permute-start(bf16[1,512,2048]{2,1,0:T(8,128)(2,1)} %get-tuple-element.55.refs_0_), channel_id=1, source_target_pairs={{0,2},{1,3},{2,0},{3,1},{4,6},{5,7},{6,4},{7,5}} | collective-permute-start | bytes 6291464 | tf_op jit(solution)/shard_map/ppermute | solution.py:206
  13.7 91.9 %collective-permute-start = (bf16[1,512,2048]{2,1,0:T(8,128)(2,1)}, bf16[1,512,2048]{2,1,0:T(8,128)(2,1)}, u32[]{:S(2)}, u32[]{:S(2)}) collective-permute-start(bf16[1,512,2048]{2,1,0:T(8,128)(2,1)} %get-tuple-element.55.refs_0_), channel_id=1, source_target_pairs={{0,1},{1,0},{2,3},{3,2},{4,5},{5,4},{6,7},{7,6}} | collective-permute-start | bytes 6291464 | tf_op jit(solution)/shard_map/ppermute | solution.py:206
  13.7 91.7 %collective-permute-start.3 = (bf16[1,512,2048]{2,1,0:T(8,128)(2,1)}, bf16[1,512,2048]{2,1,0:T(8,128)(2,1)}, u32[]{:S(2)}, u32[]{:S(2)}) collective-permute-start(bf16[1,512,2048]{2,1,0:T(8,128)(2,1)} %get-tuple-element.53.refs_3_), channel_id=1, source_target_pairs={{0,1},{1,0},{2,3},{3,2},{4,5},{5,4},{6,7},{7,6}} | collective-permute-start | bytes 6291464 | tf_op jit(solution)/shard_map/ppermute | solution.py:206
  14.2 91.4 %collective-permute-start.2 = (bf16[1,512,2048]{2,1,0:T(8,128)(2,1)}, bf16[1,512,2048]{2,1,0:T(8,128)(2,1)}, u32[]{:S(2)}, u32[]{:S(2)}) collective-permute-start(bf16[1,512,2048]{2,1,0:T(8,128)(2,1)} %get-tuple-element.54.refs_2_), channel_id=1, source_target_pairs={{0,1},{1,0},{2,3},{3,2},{4,5},{5,4},{6,7},{7,6}} | collective-permute-start | bytes 6291464 | tf_op jit(solution)/shard_map/ppermute | solution.py:206
  19.3 86.3 %collective-permute-start.1 = (bf16[3,512,2048]{2,1,0:T(8,128)(2,1)}, bf16[3,512,2048]{2,1,0:T(8,128)(2,1)}, u32[]{:S(2)}, u32[]{:S(2)}) collective-permute-start(bf16[3,512,2048]{2,1,0:T(8,128)(2,1)} %fusion.2.refs_1_), channel_id=1, source_target_pairs={{0,1},{1,0},{2,3},{3,2},{4,5},{5,4},{6,7},{7,6}} | collective-permute-start | bytes 18874376 | tf_op jit(solution)/shard_map/ppermute | solution.py:206
  104.0 137.9 %collective-permute-start.5 = (bf16[3,512,2048]{2,1,0:T(8,128)(2,1)}, bf16[3,512,2048]{2,1,0:T(8,128)(2,1)}, u32[]{:S(2)}, u32[]{:S(2)}) collective-permute-start(bf16[3,512,2048]{2,1,0:T(8,128)(2,1)} %fusion.2.refs_1_), channel_id=1, source_target_pairs={{0,2},{1,3},{2,0},{3,1},{4,6},{5,7},{6,4},{7,5}} | collective-permute-start | bytes 18874376 | tf_op jit(solution)/shard_map/ppermute | solution.py:206
  105.4 138.5 %collective-permute-start.7 = (bf16[1,512,2048]{2,1,0:T(8,128)(2,1)}, bf16[1,512,2048]{2,1,0:T(8,128)(2,1)}, u32[]{:S(2)}, u32[]{:S(2)}) collective-permute-start(bf16[1,512,2048]{2,1,0:T(8,128)(2,1)} %collective-permute-done.4.refs_4_), channel_id=1, source_target_pairs={{0,1},{1,0},{2,3},{3,2},{4,5},{5,4},{6,7},{7,6}} | collective-permute-start | bytes 6291464 | tf_op jit(solution)/shard_map/ppermute | solution.py:206
  241.9 93.3 %collective-permute-start.6 = (bf16[3,512,2048]{2,1,0:T(8,128)(2,1)}, bf16[3,512,2048]{2,1,0:T(8,128)(2,1)}, u32[]{:S(2)}, u32[]{:S(2)}) collective-permute-start(bf16[3,512,2048]{2,1,0:T(8,128)(2,1)} %collective-permute-done.5.refs_0_), channel_id=1, source_target_pairs={{0,1},{1,0},{2,3},{3,2},{4,5},{5,4},{6,7},{7,6}} | collective-permute-start | bytes 18874376 | tf_op jit(solution)/shard_map/ppermute | solution.py:206
  241.9 138.0 %collective-permute-start.9 = (bf16[1,512,2048]{2,1,0:T(8,128)(2,1)}, bf16[1,512,2048]{2,1,0:T(8,128)(2,1)}, u32[]{:S(2)}, u32[]{:S(2)}) collective-permute-start(bf16[1,512,2048]{2,1,0:T(8,128)(2,1)} %get-tuple-element.53.refs_3_), channel_id=1, source_target_pairs={{0,2},{1,3},{2,0},{3,1},{4,6},{5,7},{6,4},{7,5}} | collective-permute-start | bytes 6291464 | tf_op jit(solution)/shard_map/ppermute | solution.py:206
  243.7 91.6 %collective-permute-start.8 = (bf16[1,512,2048]{2,1,0:T(8,128)(2,1)}, bf16[1,512,2048]{2,1,0:T(8,128)(2,1)}, u32[]{:S(2)}, u32[]{:S(2)}) collective-permute-start(bf16[1,512,2048]{2,1,0:T(8,128)(2,1)} %get-tuple-element.54.refs_2_), channel_id=1, source_target_pairs={{0,2},{1,3},{2,0},{3,1},{4,6},{5,7},{6,4},{7,5}} | collective-permute-start | bytes 6291464 | tf_op jit(solution)/shard_map/ppermute | solution.py:206
  335.2 45.3 %collective-permute-start.11 = (bf16[1,512,2048]{2,1,0:T(8,128)(2,1)}, bf16[1,512,2048]{2,1,0:T(8,128)(2,1)}, u32[]{:S(2)}, u32[]{:S(2)}) collective-permute-start(bf16[1,512,2048]{2,1,0:T(8,128)(2,1)} %collective-permute-done.8.refs_0_), channel_id=1, source_target_pairs={{0,1},{1,0},{2,3},{3,2},{4,5},{5,4},{6,7},{7,6}} | collective-permute-start | bytes 6291464 | tf_op jit(solution)/shard_map/ppermute | solution.py:206
  380.0 31.7 %collective-permute-start.10 = (bf16[1,512,2048]{2,1,0:T(8,128)(2,1)}, bf16[1,512,2048]{2,1,0:T(8,128)(2,1)}, u32[]{:S(2)}, u32[]{:S(2)}) collective-permute-start(bf16[1,512,2048]{2,1,0:T(8,128)(2,1)} %collective-permute-done.9.refs_0_), channel_id=1, source_target_pairs={{0,1},{1,0},{2,3},{3,2},{4,5},{5,4},{6,7},{7,6}} | collective-permute-start | bytes 6291464 | tf_op jit(solution)/shard_map/ppermute | solution.py:206
